TPU v7x, 32 devices: a 4x2x2 block of a 4x4x8 slice. The times are simulated.
32 devices in a mesh: dp: 4 (over y, z), tp: 8 (over x, core).
Axes of the slice: x: 4, y: 2, z: 2, core: 2. Of those that a mesh axis runs over, the one named last changes fastest.
The devices are a block of a 4x4x8 slice.
Arguments:
- x: bfloat16 [512, 4096], P('dp'), parts along dimension 0
- g_attn: bfloat16 [2, 4096], replicated
- w_qkv: bfloat16 [2, 4096, 6144], P(None, None, 'tp')
- w_o: bfloat16 [2, 4096, 4096], P(None, 'tp')
- g_mlp: bfloat16 [2, 4096], replicated
- w_gate: bfloat16 [2, 4096, 14336], P(None, None, 'tp')
- w_up: bfloat16 [2, 4096, 14336], P(None, None, 'tp')
- w_down: bfloat16 [2, 14336, 4096], P(None, 'tp')
- k_cache: bfloat16 [2, 512, 128, 8, 128], P(None, 'dp', None, 'tp'), parts along dimension 1
- v_cache: bfloat16 [2, 512, 128, 8, 128], P(None, 'dp', None, 'tp'), parts along dimension 1
- lengths: int32 [512], P('dp'), parts along dimension 0
Outputs:
- output: bfloat16 [512, 4096], P('dp'), parts along dimension 0
There are 4 independent parts. A program takes and returns all parts, laid end to end along the dimension named above; an argument that names none is the same for every part.
All inputs are finite; a program needn't handle non-finite values.
Results may differ from a plain program's by a relative error of at most 0.02.
Values are sent between devices in bfloat16 or wider.
A program may use at most 768 MiB of HBM per device.

v0:
```python
import jax
import jax.numpy as jnp
from jax import lax
from jax.sharding import PartitionSpec as P

EPS = 1e-5
ROPE_THETA = 500000.0


def _rmsnorm(x, g):
    xf = x.astype(jnp.float32)
    r = lax.rsqrt(jnp.mean(xf * xf, axis=-1, keepdims=True) + EPS)
    return (xf * r * g.astype(jnp.float32)).astype(jnp.bfloat16)


def _rope(t, pos):
    hd = t.shape[-1]
    half = hd // 2
    inv = ROPE_THETA ** (-jnp.arange(half, dtype=jnp.float32) * 2.0 / hd)
    ang = pos.astype(jnp.float32)[:, None] * inv[None, :]
    shape = (pos.shape[0],) + (1,) * (t.ndim - 2) + (half,)
    c = jnp.cos(ang).reshape(shape)
    s = jnp.sin(ang).reshape(shape)
    tf = t.astype(jnp.float32)
    t1, t2 = tf[..., :half], tf[..., half:]
    return jnp.concatenate([t1 * c - t2 * s, t2 * c + t1 * s], axis=-1).astype(jnp.bfloat16)


def _attention(q, k_new, v_new, kc, vc, lengths):
    scale = q.shape[-1] ** -0.5
    s_c = jnp.einsum('bjgd,bsjd->bjgs', q, kc, preferred_element_type=jnp.float32) * scale
    mask = jnp.arange(kc.shape[1])[None, :] < lengths[:, None]
    s_c = jnp.where(mask[:, None, None, :], s_c, -jnp.inf)
    s_n = jnp.einsum('bjgd,bjd->bjg', q, k_new, preferred_element_type=jnp.float32) * scale
    m = jnp.maximum(jnp.max(s_c, axis=-1), s_n)
    p_c = jnp.exp(s_c - m[..., None])
    p_n = jnp.exp(s_n - m)
    den = jnp.sum(p_c, axis=-1) + p_n
    o = jnp.einsum('bjgs,bsjd->bjgd', p_c.astype(jnp.bfloat16), vc, preferred_element_type=jnp.float32)
    o = o + p_n[..., None] * v_new.astype(jnp.float32)[:, :, None, :]
    return o / den[..., None]


def solution(mesh):
    def body(x, g_attn, w_qkv, w_o, g_mlp, w_gate, w_up, w_down, k_cache, v_cache, lengths):
        n = x.shape[0]
        kvl, hd = k_cache.shape[3], k_cache.shape[4]
        grp = w_o.shape[1] // hd // kvl
        for l in range(w_qkv.shape[0]):
            a = _rmsnorm(x, g_attn[l])
            qkv = jnp.dot(a, w_qkv[l], preferred_element_type=jnp.float32).astype(jnp.bfloat16)
            qkv = qkv.reshape(n, kvl, grp + 2, hd)
            q = _rope(qkv[:, :, :grp], lengths)
            k = _rope(qkv[:, :, grp], lengths)
            att = _attention(q, k, qkv[:, :, grp + 1], k_cache[l], v_cache[l], lengths)
            att = att.astype(jnp.bfloat16).reshape(n, kvl * grp * hd)
            o = jnp.dot(att, w_o[l], preferred_element_type=jnp.float32).astype(jnp.bfloat16)
            h = (x.astype(jnp.float32) + lax.psum(o, 'tp').astype(jnp.float32)).astype(jnp.bfloat16)
            b = _rmsnorm(h, g_mlp[l])
            gate = jnp.dot(b, w_gate[l], preferred_element_type=jnp.float32)
            up = jnp.dot(b, w_up[l], preferred_element_type=jnp.float32)
            act = (jax.nn.silu(gate) * up).astype(jnp.bfloat16)
            m = jnp.dot(act, w_down[l], preferred_element_type=jnp.float32).astype(jnp.bfloat16)
            x = (h.astype(jnp.float32) + lax.psum(m, 'tp').astype(jnp.float32)).astype(jnp.bfloat16)
        return x

    col = P(None, None, 'tp')
    row = P(None, 'tp', None)
    cache = P(None, 'dp', None, 'tp', None)
    return jax.shard_map(body, mesh=mesh,
                         in_specs=(P('dp', None), P(), col, row, P(), col, col, row, cache, cache, P('dp')),
                         out_specs=P('dp', None), check_vma=False)
```

profile of v0, /device:TPU:81, one launch (start us, length us, event | category | flops | bytes accessed | tf_op | source)
XLA Modules:
  0.0 326.0 jit_solution(8164753408166255470)
XLA Ops:
  6.6 0.7 convert_element_type.170
  7.2 0.7 iota_compare_fusion
  8.0 1.5 fusion.50
  9.5 0.8 slice_convert_fusion.3
  10.3 4.2 %fusion.66 = bf16[128,768]{1,0:T(8,128)(2,1)S(1)} fusion(bf16[2,4096,768]{2,1,0:T(8,128)(2,1)} %param.13, bf16[128,4096]{1,0:T(8,128)(2,1)} %param.11, f32[4096]{0:T(1024)S(1)} %bitcast.167, f32[128]{0:T(128)S(1)} %add_rsqrt_fusion.3), kind=kOutput, calls=%fused_computation.72 | convolution fusion | flops 807501824 | bytes 7553536 | tf_op jit(solution)/shard_map/dot_general | solution.py:51
  14.9 0.3 multiply_cosine_fusion
  15.6 0.3 fusion.112
  16.1 0.3 fusion.149
  16.4 4.5 %fusion.147 = (f32[128,4]{1,0:T(8,128)S(1)}, f32[128,4,128]{2,1,0:T(4,128)S(1)}) fusion(bf16[128,4,128]{2,1,0:T(4,128)(2,1)S(1)} %pad_maximum_fusion, bf16[2,128,128,1,128]{4,2,1,3,0:T(8,128)(2,1)} %bitcast.168, pred[128,128]{1,0:T(8,128)(4,1)S(1)} %iota_compare_fusion), kind=kOutput, calls=%fused_computation.164 | convolution fusion | flops 16973312 | bytes 4605952 | tf_op jit(solution)/shard_map/bjgd,bsjd->bjgs/dot_general | solution.py:31
  21.0 0.4 fusion.100
  21.4 3.5 %fusion.87 = bf16[128,4,128]{2,1,0:T(4,128)(2,1)S(1)} fusion(bf16[2,128,128,1,128]{4,2,1,3,0:T(8,128)(2,1)} %bitcast.170, f32[128,4,128]{2,1,0:T(4,128)S(1)} %get-tuple-element.32, f32[128,4]{1,0:T(8,128)S(1)} %get-tuple-element.11, f32[128,128]{1,0:T(8,128)S(1)} %copy.21, f32[128,4]{1,0:T(8,128)S(1)} %get-tuple-element.12, ...), kind=kOutput, calls=%fused_computation.87 | convolution fusion | flops 17170432 | bytes 4659200 | tf_op jit(solution)/shard_map/bjgs,bsjd->bjgd/dot_general | solution.py:39
  24.9 4.0 %convolution_convert_fusion.1 = bf16[128,4096]{1,0:T(8,128)(2,1)} fusion(bf16[2,512,4096]{2,1,0:T(8,128)(2,1)} %param.14, bf16[16,8,4,128]{3,2,1,0:T(4,128)(2,1)S(1)} %bitcast.172), kind=kOutput, calls=%fused_computation.27 | convolution fusion | flops 537395200 | bytes 5373952 | tf_op jit(solution)/shard_map/dot_general | solution.py:57
  29.0 58.4 %all-reduce.5.cloned.1.call-done = bf16[128,4096]{1,0:T(8,128)(2,1)} async-done(((bf16[128,4096]{1,0:T(8,128)(2,1)}), bf16[128,4096]{1,0:T(8,128)(2,1)}) %all-reduce.5.cloned.1.call-update) | async-done | bytes 1048592 | tf_op jit(solution)/shard_map/psum | solution.py:58
  87.4 1.7 fusion.54
  89.1 6.5 %fusion.10 = f32[128,1792]{1,0:T(8,128)S(1)} fusion(bf16[2,4096,1792]{2,1,0:T(8,128)(2,1)} %param.16, bf16[128,4096]{1,0:T(8,128)(2,1)S(1)} %get-tuple-element.10, f32[4096]{0:T(1024)S(1)} %bitcast.165, f32[128]{0:T(128)S(1)} %add_rsqrt_fusion.2), kind=kOutput, calls=%fused_computation.10 | convolution fusion | flops 1881145344 | bytes 16663040 | tf_op jit(solution)/shard_map/dot_general | solution.py:60
  95.6 12.9 %fusion.24 = bf16[128,4096]{1,0:T(8,128)(2,1)} fusion(bf16[2,1792,4096]{2,1,0:T(8,128)(2,1)} %param.18, bf16[2,4096,1792]{2,1,0:T(8,128)(2,1)} %param.17, f32[128,1792]{1,0:T(8,128)S(1)} %fusion.10, bf16[128,4096]{1,0:T(8,128)(2,1)S(1)} %get-tuple-element.10, f32[4096]{0:T(1024)S(1)} %bitcast.166, f32[128]{0:T(128)S(1)} %add_rsqrt_fusion.2), kind=kOutput, calls=%fused_computation.24 | convolution fusion | flops 3762094080 | bytes 32391680 | tf_op jit(solution)/shard_map/dot_general | solution.py:63
  108.6 0.2 all-reduce.9.cloned.1.call-start
  108.9 55.4 %all-reduce.7.cloned.1.call-done = bf16[128,4096]{1,0:T(8,128)(2,1)} async-done(((bf16[128,4096]{1,0:T(8,128)(2,1)}), bf16[128,4096]{1,0:T(8,128)(2,1)}) %all-reduce.7.cloned.1.call-update) | async-done | bytes 1048592 | tf_op jit(solution)/shard_map/psum | solution.py:64
  164.3 1.6 fusion.58
  165.9 4.2 %fusion.69 = bf16[128,768]{1,0:T(8,128)(2,1)S(1)} fusion(bf16[2,4096,768]{2,1,0:T(8,128)(2,1)} %param.13, f32[4096]{0:T(1024)S(1)} %bitcast.164, f32[128]{0:T(128)S(1)} %add_rsqrt_fusion.1, bf16[128,4096]{1,0:T(8,128)(2,1)S(1)} %get-tuple-element.10, bf16[128,4096]{1,0:T(8,128)(2,1)} %all-reduce.7.cloned.1.call-done), kind=kOutput, calls=%fused_computation.73 | convolution fusion | flops 809598976 | bytes 8602112 | tf_op jit(solution)/shard_map/dot_general | solution.py:51
  171.0 0.3 fusion.114
  171.5 4.5 %fusion.148 = (f32[128,4]{1,0:T(8,128)S(1)}, f32[128,4,128]{2,1,0:T(4,128)S(1)}) fusion(bf16[128,4,128]{2,1,0:T(4,128)(2,1)S(1)} %pad_maximum_fusion.1, bf16[2,128,128,1,128]{4,2,1,3,0:T(8,128)(2,1)} %bitcast.169, pred[128,128]{1,0:T(8,128)(4,1)S(1)} %iota_compare_fusion), kind=kOutput, calls=%fused_computation.165 | convolution fusion | flops 16973312 | bytes 4605952 | tf_op jit(solution)/shard_map/bjgd,bsjd->bjgs/dot_general | solution.py:31
  176.0 0.3 fusion.150
  176.3 0.4 fusion.102
  176.7 3.5 %fusion.85 = bf16[128,4,128]{2,1,0:T(4,128)(2,1)S(1)} fusion(bf16[2,128,128,1,128]{4,2,1,3,0:T(8,128)(2,1)} %bitcast.171, f32[128,4,128]{2,1,0:T(4,128)S(1)} %get-tuple-element.34, f32[128,4]{1,0:T(8,128)S(1)} %get-tuple-element.7, f32[128,128]{1,0:T(8,128)S(1)} %copy.26, f32[128,4]{1,0:T(8,128)S(1)} %get-tuple-element.8, f32[128,4]{1,0:T(8,128)S(1)} %multiply_maximum_fusion), kind=kOutput, calls=%fused_computation.85 | convolution fusion | flops 17170432 | bytes 4659200 | tf_op jit(solution)/shard_map/bjgs,bsjd->bjgd/dot_general | solution.py:39
  180.2 4.0 %convolution_convert_fusion = bf16[128,4096]{1,0:T(8,128)(2,1)} fusion(bf16[2,512,4096]{2,1,0:T(8,128)(2,1)} %param.14, bf16[16,8,4,128]{3,2,1,0:T(4,128)(2,1)S(1)} %bitcast.173), kind=kOutput, calls=%fused_computation.26 | convolution fusion | flops 537395200 | bytes 5373952 | tf_op jit(solution)/shard_map/dot_general | solution.py:57
  184.3 55.6 %all-reduce.9.cloned.1.call-done = bf16[128,4096]{1,0:T(8,128)(2,1)} async-done(((bf16[128,4096]{1,0:T(8,128)(2,1)}), bf16[128,4096]{1,0:T(8,128)(2,1)}) %all-reduce.9.cloned.1.call-update) | async-done | bytes 1048592 | tf_op jit(solution)/shard_map/psum | solution.py:58
  239.9 1.8 fusion.62
  241.8 6.5 %fusion.4 = f32[128,1792]{1,0:T(8,128)S(1)} fusion(bf16[2,4096,1792]{2,1,0:T(8,128)(2,1)} %param.16, bf16[128,4096]{1,0:T(8,128)(2,1)S(1)} %get-tuple-element.6, f32[4096]{0:T(1024)S(1)} %bitcast.162, f32[128]{0:T(128)S(1)} %add_rsqrt_fusion), kind=kOutput, calls=%fused_computation.4 | convolution fusion | flops 1881145344 | bytes 16663040 | tf_op jit(solution)/shard_map/dot_general | solution.py:60
  248.3 12.9 %fusion.27 = bf16[128,4096]{1,0:T(8,128)(2,1)} fusion(bf16[2,1792,4096]{2,1,0:T(8,128)(2,1)} %param.18, bf16[2,4096,1792]{2,1,0:T(8,128)(2,1)} %param.17, f32[128,1792]{1,0:T(8,128)S(1)} %fusion.4, bf16[128,4096]{1,0:T(8,128)(2,1)S(1)} %get-tuple-element.6, f32[4096]{0:T(1024)S(1)} %bitcast.163, f32[128]{0:T(128)S(1)} %add_rsqrt_fusion), kind=kOutput, calls=%fused_computation.25 | convolution fusion | flops 3762094080 | bytes 32391680 | tf_op jit(solution)/shard_map/dot_general | solution.py:63
  261.3 55.8 %all-reduce.11.cloned.1.call-done = bf16[128,4096]{1,0:T(8,128)(2,1)} async-done(((bf16[128,4096]{1,0:T(8,128)(2,1)}), bf16[128,4096]{1,0:T(8,128)(2,1)}) %all-reduce.11.cloned.1.call-update) | async-done | bytes 1048592 | tf_op jit(solution)/shard_map/psum | solution.py:64
  317.0 2.4 fusion.65
  (43 shorter events, 2.4 us)
Async XLA Ops:
  6.5 80.9 %all-reduce.5.cloned.1.call-start = ((), (), s32[]{:S(2)}) async-start(), calls=%async_computation | async-start | bytes 2097152 | tf_op jit(solution)/shard_map/psum | solution.py:58
  24.9 4.1 %copy-start.2 = (bf16[2,4096]{1,0:T(2,128)(2,1)S(1)}, bf16[2,4096]{1,0:T(2,128)(2,1)}, u32[]{:S(2)}) copy-start(bf16[2,4096]{1,0:T(2,128)(2,1)} %param.15) | copy-start | bytes 49156
  24.9 62.6 %copy-start.1 = (bf16[128,4096]{1,0:T(8,128)(2,1)S(1)}, bf16[128,4096]{1,0:T(8,128)(2,1)}, u32[]{:S(2)}) copy-start(bf16[128,4096]{1,0:T(8,128)(2,1)} %param.11) | copy-start | bytes 3145732
  28.9 135.3 %all-reduce.7.cloned.1.call-start = ((), (), s32[]{:S(2)}) async-start(), calls=%async_computation.1 | async-start | bytes 2097152 | tf_op jit(solution)/shard_map/psum | solution.py:64
  108.6 131.3 %all-reduce.9.cloned.1.call-start = ((), (), s32[]{:S(2)}) async-start(), calls=%async_computation.2 | async-start | bytes 2097152 | tf_op jit(solution)/shard_map/psum | solution.py:58
  180.2 59.7 %copy-start = (bf16[128,4096]{1,0:T(8,128)(2,1)S(1)}, bf16[128,4096]{1,0:T(8,128)(2,1)}, u32[]{:S(2)}) copy-start(bf16[128,4096]{1,0:T(8,128)(2,1)} %all-reduce.7.cloned.1.call-done) | copy-start | bytes 3145732
  184.2 132.8 %all-reduce.11.cloned.1.call-start = ((), (), s32[]{:S(2)}) async-start(), calls=%async_computation.3 | async-start | bytes 2097152 | tf_op jit(solution)/shard_map/psum | solution.py:64
Sparse Core Ops, SparseCore 0:
  29.0 58.3 all-reduce.4
  108.7 55.4 all-reduce.6
  184.4 55.5 all-reduce.8
  261.4 55.5 all-reduce.10
where the time goes:
time: 327 us; the launch traced here: 326 us
  waiting for transfers between devices  225 us (69%)
  matrix products  71.7 us (22%)
  other arithmetic  14 us (4%)
  between operations  13.5 us (4%)
    psum x2, waiting for transfers between devices, body(): lax.psum(o, 'tp').astype(jnp.float32)  114 us
    psum x2, waiting for transfers between devices, body(): lax.psum(m, 'tp').astype(jnp.float32)  111 us
    dot_general x2, matrix products, body(): jnp.dot(act, w_down[l], preferred_element_type=jnp.float32)  25.8 us
    dot_general x2, matrix products, body(): gate = jnp.dot(b, w_gate[l], preferred_element_type=jnp.float32)  13 us
    dot_general x2, matrix products, _attention(): jnp.einsum('bjgd,bsjd->bjgs', q, kc, preferred_element_type=jnp.float32)  9.08 us
    dot_general x2, matrix products, body(): jnp.dot(a, w_qkv[l], preferred_element_type=jnp.float32)  8.39 us
    dot_general x2, matrix products, body(): jnp.dot(att, w_o[l], preferred_element_type=jnp.float32)  7.94 us
    dot_general x2, matrix products, _attention(): jnp.einsum('bjgs,bsjd->bjgd', p_c.astype(jnp.bfloat16), vc, preferred_ele...  6.94 us
  transfers between devices with their start and end apart: 4, of which 4 were waited for; matrix products, arithmetic and copies ran while one was open for 0% of the time, Pallas kernels for 0%

commit v1 on v0

v1 whole, which is shorter than its diff:
```python
import functools

import jax
import jax.numpy as jnp
import numpy as np
from jax import lax
from jax.experimental import pallas as pl
from jax.experimental.pallas import tpu as pltpu
from jax.sharding import PartitionSpec as P

EPS = 1e-5
ROPE_THETA = 500000.0
F32 = jnp.float32
BF16 = jnp.bfloat16
SLOTS = 8
SLOTS_PER_STEP = 2
RS_ORDER = (2, 1, 3, 0)
AG_ORDER = (0, 3, 1, 2)


def _dot(a, b):
    return jnp.dot(a, b, preferred_element_type=F32)


def _dot_nt(a, b):
    return lax.dot_general(a, b, (((1,), (1,)), ((), ())), preferred_element_type=F32)


def _kernel(dims, x_hbm, ga_ref, wqkv_hbm, wo_hbm, gm_ref, wg_hbm, wu_hbm, wd_hbm, kc_hbm, vc_hbm, len_ref, inv_ref,
            y_hbm,
            wq, wo, wg, wu, wd, kv, hbuf, abuf, part, pair_in, relay_in, rs_in, sown, pool, act, lrow, cosb, sinb, att,
            s_x, s_q, s_o, s_g, s_u, s_d, s_kv, s_y,
            pr_s, pr_r, rl_s, rl_r, rs_s, rs_r, ag_s, ag_r, ad_s, ad_r):
    L, n, D, NQ, KO, F, S, hd, R = dims
    NB = 2 * R
    BW = D // NB
    PW = BW // 2
    grp = KO // hd
    T = n // SLOTS
    LW = 128
    NR = n * grp
    qrow, krow, vrow, arow, prow = (pool.at[pl.ds(i * NR, NR)] for i in range(5))
    tp = lax.axis_index("tp")
    x = tp // 2
    c = tp % 2
    right = {"tp": ((x + 1) % R) * 2 + c}
    left = {"tp": ((x + R - 1) % R) * 2 + c}
    partner = {"tp": x * 2 + (1 - c)}
    MESH = pl.DeviceIdType.MESH

    def chip(off):
        return (x + off) % R

    def cols(start, size):
        return pl.ds(pl.multiple_of(start, 128), size)

    def rows(start, size):
        return pl.ds(pl.multiple_of(start, 128), size)

    def cp_x(p):
        return pltpu.make_async_copy(x_hbm.at[:, cols(p * PW, PW)], hbuf.at[p], s_x.at[p])

    def cp_q(l, j):
        return pltpu.make_async_copy(wqkv_hbm.at[l, rows(j * BW, BW), :], wq.at[rows(j * BW, BW), :], s_q.at[j])

    def cp_o(l, j):
        return pltpu.make_async_copy(wo_hbm.at[l, :, cols(j * BW, BW)], wo.at[:, cols(j * BW, BW)], s_o.at[j])

    def cp_g(l, j):
        return pltpu.make_async_copy(wg_hbm.at[l, rows(j * BW, BW), :], wg.at[rows(j * BW, BW), :], s_g.at[j])

    def cp_u(l, j):
        return pltpu.make_async_copy(wu_hbm.at[l, rows(j * BW, BW), :], wu.at[rows(j * BW, BW), :], s_u.at[j])

    def cp_d(l, j):
        return pltpu.make_async_copy(wd_hbm.at[l, :, cols(j * BW, BW)], wd.at[:, cols(j * BW, BW)], s_d.at[j])

    def cp_k(l, s):
        return pltpu.make_async_copy(kc_hbm.at[l, pl.ds(s * T, T)], kv.at[s], s_kv.at[s])

    def cp_v(l, s):
        return pltpu.make_async_copy(vc_hbm.at[l, pl.ds(s * T, T)], kv.at[s], s_kv.at[s])

    def blocks(order):
        return [cc * R + chip(o) for o in order for cc in range(2)]

    barrier = pltpu.get_barrier_semaphore()
    for d in (partner, right, left):
        pl.semaphore_signal(barrier, inc=1, device_id=d, device_id_type=MESH)

    for p in range(2 * NB):
        cp_x(p).start()
    for j in blocks(AG_ORDER):
        cp_q(0, j).start()
    for s in range(SLOTS):
        cp_k(0, s).start()
    for j in range(NB):
        cp_o(0, j).start()

    lcol = jnp.broadcast_to(len_ref[...].astype(F32), (hd, n)).T
    ang = lcol * inv_ref[...]
    lane = lax.broadcasted_iota(jnp.int32, (n, hd), 1)
    cosb[...] = jnp.cos(ang)
    sn = jnp.sin(ang)
    sinb[...] = jnp.where(lane < hd // 2, -sn, sn)
    for g in range(grp):
        lrow[pl.ds(g, n, stride=grp), :] = lcol

    for p in range(2 * NB):
        cp_x(p).wait()

    def gain(ref, l, p):
        g = ref[0:1, cols(p * PW, PW)]
        for i in range(1, L):
            g = jnp.where(l == i, ref[i:i + 1, cols(p * PW, PW)].astype(F32), g.astype(F32))
        return g.astype(F32)

    def norm(l, ref):
        def sq(p, s):
            v = hbuf[p].astype(F32)
            return s + v * v
        s = lax.fori_loop(0, 2 * NB, sq, jnp.zeros((n, PW), F32))
        r = lax.rsqrt(jnp.sum(s, axis=-1, keepdims=True) * (1.0 / D) + EPS)

        def put(p, carry):
            abuf[p] = (hbuf[p].astype(F32) * r * gain(ref, l, p)).astype(BF16)
            return carry
        lax.fori_loop(0, 2 * NB, put, 0)

    def ag_chip(i):
        return chip(jnp.where(i == 0, AG_ORDER[0], jnp.where(i == 1, AG_ORDER[1], jnp.where(i == 2, AG_ORDER[2], AG_ORDER[3]))))

    def group_dot(w, b, n0, nw):
        s = None
        for cc in range(2):
            for h in range(2):
                d = _dot(abuf[cc * NB + b * 2 + h], w[rows((cc * R + b) * BW + h * PW, PW), n0:n0 + nw])
                s = d if s is None else s + d
        return s

    def unit(i):
        return pl.ds(i * n, n)

    def accumulate(u, d):
        for k in range(d.shape[1] // LW):
            pool[unit(u + k), :] += d[:, k * LW:(k + 1) * LW]

    def tiles(width):
        t = []
        n0 = 0
        while n0 < width:
            t.append((n0, min(256, width - n0)))
            n0 += 256
        return t

    def remote(src, dst, ss, rs, dev):
        return pltpu.make_async_remote_copy(src_ref=src, dst_ref=dst, send_sem=ss, recv_sem=rs, device_id=dev,
                                            device_id_type=MESH)

    def all_reduce(block, wait_w):
        pair = []
        for i, off in enumerate(RS_ORDER):
            j = (1 - c) * R + chip(off)
            wait_w(j)
            o = block(j).astype(BF16)
            part[j, 0] = o[:, :PW]
            part[j, 1] = o[:, PW:]
            d = remote(part.at[j], pair_in.at[i], pr_s.at[i], pr_r.at[i], partner)
            d.start()
            pair.append(d)
        sends = []
        for i, off in enumerate(RS_ORDER):
            j = c * R + chip(off)
            wait_w(j)
            o = block(j).astype(BF16).astype(F32)
            pair[i].wait_recv()
            s0 = o[:, :PW] + pair_in[i, 0].astype(F32)
            s1 = o[:, PW:] + pair_in[i, 1].astype(F32)
            if i == 3:
                sown[0] = s0
                sown[1] = s1
                continue
            part[j, 0] = s0.astype(BF16)
            part[j, 1] = s1.astype(BF16)
            if i == 0:
                ra = remote(part.at[j, 0], relay_in.at[0], rl_s.at[0], rl_r.at[0], right)
                rb = remote(part.at[j, 1], relay_in.at[1], rl_s.at[1], rl_r.at[1], left)
                ra.start()
                rb.start()
            elif i == 1:
                d0 = remote(part.at[j, 1], rs_in.at[0], rs_s.at[0], rs_r.at[0], right)
                d0.start()
            else:
                d1 = remote(part.at[j, 0], rs_in.at[1], rs_s.at[1], rs_r.at[1], left)
                d1.start()
        jr = c * R + chip(1)
        jl = c * R + chip(3)
        ra.wait_recv()
        part[jr, 0] = (part[jr, 0].astype(F32) + relay_in[0].astype(F32)).astype(BF16)
        d2 = remote(part.at[jr, 0], rs_in.at[2], rs_s.at[2], rs_r.at[2], right)
        d2.start()
        rb.wait_recv()
        part[jl, 1] = (part[jl, 1].astype(F32) + relay_in[1].astype(F32)).astype(BF16)
        d3 = remote(part.at[jl, 1], rs_in.at[3], rs_s.at[3], rs_r.at[3], left)
        d3.start()
        d1.wait_recv()
        d0.wait_recv()
        own = c * NB + x * 2
        t0 = hbuf[own].astype(F32)
        t1 = hbuf[own + 1].astype(F32)
        s0 = sown[0] + rs_in[1].astype(F32)
        s1 = sown[1] + rs_in[0].astype(F32)
        d2.wait_recv()
        hbuf[own] = (t0 + (s0 + rs_in[2].astype(F32))).astype(BF16)
        d3.wait_recv()
        hbuf[own + 1] = (t1 + (s1 + rs_in[3].astype(F32))).astype(BF16)

        def piece(cc, b, h):
            return hbuf.at[cc * NB + b * 2 + h]

        lb, rb_, ob = chip(3), chip(1), chip(2)
        a0 = remote(piece(c, x, 0), piece(c, x, 0), ag_s.at[0], ag_r.at[0], right)
        a1 = remote(piece(c, x, 1), piece(c, x, 1), ag_s.at[1], ag_r.at[1], left)
        a2 = remote(piece(c, x, 1), piece(c, x, 1), ag_s.at[2], ag_r.at[2], right)
        a3 = remote(piece(c, x, 0), piece(c, x, 0), ag_s.at[3], ag_r.at[3], left)
        own2 = hbuf.at[pl.ds(own, 2)]
        p0 = remote(own2, own2, ad_s.at[0], ad_r.at[0], partner)
        for d in (a0, a1, a2, a3, p0):
            d.start()

        def fwd(k, ref):
            d = remote(ref, ref, ad_s.at[k], ad_r.at[k], partner)
            d.start()
            return d

        a0.wait_recv()
        a4 = remote(piece(c, lb, 0), piece(c, lb, 0), ag_s.at[4], ag_r.at[4], right)
        a4.start()
        f1 = fwd(1, piece(c, lb, 0))
        a1.wait_recv()
        a5 = remote(piece(c, rb_, 1), piece(c, rb_, 1), ag_s.at[5], ag_r.at[5], left)
        a5.start()
        f2 = fwd(2, piece(c, rb_, 1))
        a2.wait_recv()
        f3 = fwd(3, piece(c, lb, 1))
        a3.wait_recv()
        f4 = fwd(4, piece(c, rb_, 0))
        a4.wait_recv()
        f5 = fwd(5, piece(c, ob, 0))
        a5.wait_recv()
        f6 = fwd(6, piece(c, ob, 1))
        for d in (p0, f1, f2, f3, f4, f5, f6):
            d.wait_recv()
        for d in pair + [ra, rb, d0, d1, d2, d3, a0, a1, a2, a3, a4, a5, p0, f1, f2, f3, f4, f5, f6]:
            d.wait_send()

    def layer(l, carry):
        more = l + 1 < L

        norm(l, ga_ref)
        pool[...] = jnp.zeros_like(pool)

        def qkv_step(i, carry):
            b = ag_chip(i)
            for cc in range(2):
                cp_q(l, cc * R + b).wait()
            for n0, nw in tiles(NQ):
                accumulate(5 * grp + n0 // LW, group_dot(wq, b, n0, nw))
            return carry
        lax.fori_loop(0, R, qkv_step, 0)

        @pl.when(l == 0)
        def _():
            for j in blocks(AG_ORDER):
                cp_g(0, j).start()
                cp_u(0, j).start()
            for j in range(NB):
                cp_d(0, j).start()

        @pl.when(more)
        def _():
            for j in blocks(AG_ORDER):
                cp_q(l + 1, j).start()

        def rope(t):
            return (t * cosb[...] + pltpu.roll(t, hd // 2, 1) * sinb[...]).astype(BF16).astype(F32)

        def head(i):
            return pool[unit(5 * grp + i), :].astype(BF16).astype(F32)

        kn = rope(head(grp))
        vn = head(grp + 1)
        for g in range(grp):
            qrow[pl.ds(g, n, stride=grp), :] = rope(head(g))
            krow[pl.ds(g, n, stride=grp), :] = kn
            vrow[pl.ds(g, n, stride=grp), :] = vn

        first = lax.broadcasted_iota(jnp.int32, (2 * grp, S), 0) < grp

        def qk_step(i, carry):
            for s2 in range(SLOTS_PER_STEP):
                s = i * SLOTS_PER_STEP + s2
                cp_k(l, s).wait()
                for t in range(0, T, 2):
                    r0 = pl.multiple_of((s * T + t) * grp, 2 * grp)
                    q8 = qrow[pl.ds(r0, 2 * grp), :].astype(BF16)
                    k2 = kv[s, t:t + 2].reshape(2 * S, hd)
                    o = _dot_nt(q8, k2)
                    arow[pl.ds(r0, 2 * grp), :] = jnp.where(first, o[:, :S], o[:, S:])
            for s2 in range(SLOTS_PER_STEP):
                cp_v(l, i * SLOTS_PER_STEP + s2).start()
            return carry
        lax.fori_loop(0, SLOTS // SLOTS_PER_STEP, qk_step, 0)

        scale = hd ** -0.5
        CH = n * grp // 4
        for ch in range(4):
            rs = slice(ch * CH, (ch + 1) * CH)
            pos = lax.broadcasted_iota(jnp.int32, (CH, S), 1).astype(F32)
            sc = jnp.where(pos < lrow[rs, :], arow[rs, :] * scale, -jnp.inf)
            s_n = jnp.sum(qrow[rs, :] * krow[rs, :], axis=-1, keepdims=True) * scale
            m = jnp.maximum(jnp.max(sc, axis=-1, keepdims=True), s_n)
            p_c = jnp.exp(sc - m)
            p_n = jnp.exp(s_n - m)
            den = jnp.sum(p_c, axis=-1, keepdims=True) + p_n
            prow[rs, :] = p_c
            krow[rs, :] = jnp.broadcast_to(den, (CH, S))
            vrow[rs, :] = vrow[rs, :] * p_n

        def pv_step(i, carry):
            for s2 in range(SLOTS_PER_STEP):
                s = i * SLOTS_PER_STEP + s2
                cp_v(l, s).wait()
                for t in range(0, T, 2):
                    r0 = pl.multiple_of((s * T + t) * grp, 2 * grp)
                    p8 = prow[pl.ds(r0, 2 * grp), :]
                    pp = jnp.concatenate([jnp.where(first, p8, 0.0), jnp.where(first, 0.0, p8)], axis=1).astype(BF16)
                    o = _dot(pp, kv[s, t:t + 2].reshape(2 * S, hd))
                    arow[pl.ds(r0, 2 * grp), :] = o

            @pl.when(more)
            def _():
                for s2 in range(SLOTS_PER_STEP):
                    cp_k(l + 1, i * SLOTS_PER_STEP + s2).start()
            return carry
        lax.fori_loop(0, SLOTS // SLOTS_PER_STEP, pv_step, 0)

        for ch in range(4):
            rs = slice(ch * CH, (ch + 1) * CH)
            arow[rs, :] = (arow[rs, :] + vrow[rs, :]) / krow[rs, :]
        for g in range(grp):
            att[:, g * hd:(g + 1) * hd] = arow[pl.ds(g, n, stride=grp), :].astype(BF16)

        @pl.when(l == 0)
        def _():
            pl.semaphore_wait(barrier, 3)

        all_reduce(lambda j: _dot(att[...], wo[:, cols(j * BW, BW)]), lambda j: cp_o(l, j).wait())

        @pl.when(more)
        def _():
            for j in range(NB):
                cp_o(l + 1, j).start()

        norm(l, gm_ref)
        pool[...] = jnp.zeros_like(pool)

        def mlp_step(i, carry):
            b = ag_chip(i)
            for cc in range(2):
                cp_g(l, cc * R + b).wait()
                cp_u(l, cc * R + b).wait()
            for k, w in enumerate((wg, wu)):
                for n0, nw in tiles(F):
                    accumulate((k * F + n0) // LW, group_dot(w, b, n0, nw))
            return carry
        lax.fori_loop(0, R, mlp_step, 0)

        @pl.when(more)
        def _():
            for j in blocks(AG_ORDER):
                cp_g(l + 1, j).start()
                cp_u(l + 1, j).start()

        for u in range(F // LW):
            act[:, u * LW:(u + 1) * LW] = (jax.nn.silu(pool[unit(u), :]) * pool[unit(F // LW + u), :]).astype(BF16)

        all_reduce(lambda j: _dot(act[...], wd[:, cols(j * BW, BW)]), lambda j: cp_d(l, j).wait())

        @pl.when(more)
        def _():
            for j in range(NB):
                cp_d(l + 1, j).start()
        return carry

    lax.fori_loop(0, L, layer, 0)

    outs = [pltpu.make_async_copy(hbuf.at[p], y_hbm.at[:, cols(p * PW, PW)], s_y.at[p]) for p in range(2 * NB)]
    for d in outs:
        d.start()
    for d in outs:
        d.wait()


def solution(mesh):
    tp = mesh.shape["tp"]

    def body(x, g_attn, w_qkv, w_o, g_mlp, w_gate, w_up, w_down, k_cache, v_cache, lengths):
        n, D = x.shape
        L, _, NQ = w_qkv.shape
        KO, F = w_o.shape[1], w_gate.shape[2]
        S, hd = k_cache.shape[2], k_cache.shape[4]
        R = tp // 2
        NB, PW, BW = tp, D // tp // 2, D // tp
        grp = KO // hd
        kc = k_cache.reshape(L, n, S, hd)
        vc = v_cache.reshape(L, n, S, hd)
        half = hd // 2
        inv = np.float32(ROPE_THETA) ** (-np.arange(half, dtype=np.float32) * np.float32(2.0) / np.float32(hd))
        inv = jnp.asarray(np.concatenate([inv, inv])[None, :].astype(np.float32))
        dims = (L, n, D, NQ, KO, F, S, hd, R)
        anyspec = pl.BlockSpec(memory_space=pl.ANY)
        vspec = pl.BlockSpec(memory_space=pltpu.VMEM)
        V = pltpu.VMEM
        DMA = pltpu.SemaphoreType.DMA
        rows = n * grp
        scratch = [
            V((D, NQ), BF16), V((KO, D), BF16), V((D, F), BF16), V((D, F), BF16), V((F, D), BF16),
            V((SLOTS, n // SLOTS, S, hd), BF16),
            V((2 * NB, n, PW), BF16), V((2 * NB, n, PW), BF16),
            V((NB, 2, n, PW), BF16), V((R, 2, n, PW), BF16), V((2, n, PW), BF16), V((4, n, PW), BF16), V((2, n, PW), F32),
            V((max(2 * F // 128, 5 * grp + NQ // 128) * n, 128), F32), V((n, F), BF16),
            V((rows, hd), F32), V((n, hd), F32), V((n, hd), F32), V((n, KO), BF16),
            DMA((2 * NB,)), DMA((NB,)), DMA((NB,)), DMA((NB,)), DMA((NB,)), DMA((NB,)), DMA((SLOTS,)), DMA((2 * NB,)),
            DMA((4,)), DMA((4,)), DMA((2,)), DMA((2,)), DMA((4,)), DMA((4,)), DMA((6,)), DMA((6,)), DMA((7,)), DMA((7,)),
        ]
        return pl.pallas_call(
            functools.partial(_kernel, dims),
            out_shape=jax.ShapeDtypeStruct((n, D), BF16),
            in_specs=[anyspec, vspec, anyspec, anyspec, vspec, anyspec, anyspec, anyspec, anyspec, anyspec, vspec, vspec],
            out_specs=anyspec,
            scratch_shapes=scratch,
            compiler_params=pltpu.CompilerParams(collective_id=0, has_side_effects=True, vmem_limit_bytes=67043328),
        )(x, g_attn, w_qkv, w_o, g_mlp, w_gate, w_up, w_down, kc, vc, lengths.reshape(1, n), inv)

    col = P(None, None, 'tp')
    row = P(None, 'tp', None)
    cache = P(None, 'dp', None, 'tp', None)
    return jax.shard_map(body, mesh=mesh,
                         in_specs=(P('dp', None), P(), col, row, P(), col, col, row, cache, cache, P('dp')),
                         out_specs=P('dp', None), check_vma=False)
```

time: 327 us -> 126 us (0.39)
  waiting for transfers between devices: 225 us -> 0 us
  Pallas kernels: 0 us -> 123 us
  matrix products: 71.7 us -> 0 us
  other arithmetic: 14 us -> 0 us
  between operations: 13.5 us -> 0.01 us
    psum x4 -> x0, waiting for transfers between devices: 225 us -> none  [the longest x2 114 us: body(): lax.psum(o, 'tp').astype(jnp.float32)]
    pallas_call x0 -> x1, Pallas kernels: none -> 123 us  [body(): pl.pallas_call(functools.partial(_kernel, dims), out_shape=jax.ShapeDtype...]
    dot_general x14 -> x0, matrix products: 71.7 us -> none  [the longest x2 25.8 us: body(): jnp.dot(act, w_down[l], preferred_element_type=jnp.float32)]
    reduce_sum x6 -> x0, other arithmetic: 7.41 us -> none  [the longest x4 6.65 us: _rmsnorm(): r = lax.rsqrt(jnp.mean(xf * xf, axis=-1, keepdims=True) + EPS)]
  transfers between devices with their start and end apart: 4 -> 0, of which waited for: 4 -> 0; matrix products, arithmetic and copies ran while one was open for 0% -> 0% of each run, Pallas kernels for 0% -> 0%
where the time goes in v1:
time: 126 us; the launch traced here: 125 us
  Pallas kernels  123 us (98%)
  local copies, waits for them, and re-layouts  2.29 us (2%)
    pallas_call x1, Pallas kernels, body(): pl.pallas_call(functools.partial(_kernel, dims), out_shape=jax.ShapeDtype...  123 us

profile of v1, /device:TPU:81, one launch (start us, length us, event | category | flops | bytes accessed | tf_op | source)
XLA Modules:
  0.0 125.3 jit_solution(14617414169473563626)
XLA Ops:
  0.0 123.0 %shard_map.118 = bf16[128,4096]{1,0:T(8,128)(2,1)} custom-call(bf16[128,4096]{1,0:T(8,128)(2,1)} %x_hbm.1, bf16[2,4096]{1,0:T(2,128)(2,1)} %ga_ref.1, bf16[2,4096,768]{2,1,0:T(8,128)(2,1)} %wqkv_hbm.1, bf16[2,512,4096]{2,1,0:T(8,128)(2,1)} %wo_hbm.1, bf16[2,4096]{1,0:T(2,128)(2,1)} %gm_ref.1, bf16[2,4096,1792]{2,1,0:T(8,128)(2,1)} %wg_hbm.1, ...), custom_call_target="tpu_custom_call" | custom-call | tf_op jit(solution)/shard_map/pallas_call | solution.py:437
  123.1 2.3 %copy.14 = bf16[128,4096]{1,0:T(8,128)(2,1)} copy(bf16[128,4096]{1,0:T(8,128)(2,1)} %shard_map.118) | data formatting | bytes 2097152

commit v2 on v0

v2 whole, which is shorter than its diff:
```python
import functools

import jax
import jax.numpy as jnp
import numpy as np
from jax import lax
from jax.experimental import pallas as pl
from jax.experimental.pallas import tpu as pltpu
from jax.sharding import PartitionSpec as P

EPS = 1e-5
ROPE_THETA = 500000.0
F32 = jnp.float32
BF16 = jnp.bfloat16
SLOTS = 8
SLOTS_PER_STEP = 2
RS_ORDER = (2, 1, 3, 0)


def _dot(a, b):
    return jnp.dot(a, b, preferred_element_type=F32)


def _dot_nt(a, b):
    return lax.dot_general(a, b, (((1,), (1,)), ((), ())), preferred_element_type=F32)


def _kernel(dims, x_hbm, ga_ref, wqkv_hbm, wo_hbm, gm_ref, wg_hbm, wu_hbm, wd_hbm, kc_hbm, vc_hbm, len_ref, inv_ref,
            y_hbm,
            wq, wo, wg, wu, wd, kv, hbuf, abuf, part, pair_in, relay_in, rs_in, sown, pool, act, lrow, cosb, sinb, att, rbuf, stat,
            s_x, s_q, s_o, s_g, s_u, s_d, s_kv, s_y,
            pr_s, pr_r, rl_s, rl_r, rs_s, rs_r, ag_s, ag_r, ad_s, ad_r, st_s, st_r):
    L, n, D, NQ, KO, F, S, hd, R = dims
    NB = 2 * R
    BW = D // NB
    PW = BW // 2
    grp = KO // hd
    T = n // SLOTS
    LW = 128
    NR = n * grp
    qrow, krow, vrow, arow, prow = (pool.at[pl.ds(i * NR, NR)] for i in range(5))
    tp = lax.axis_index("tp")
    x = tp // 2
    c = tp % 2
    right = {"tp": ((x + 1) % R) * 2 + c}
    left = {"tp": ((x + R - 1) % R) * 2 + c}
    partner = {"tp": x * 2 + (1 - c)}
    MESH = pl.DeviceIdType.MESH

    def chip(off):
        return (x + off) % R

    def cols(start, size):
        return pl.ds(pl.multiple_of(start, 128), size)

    def rows(start, size):
        return pl.ds(pl.multiple_of(start, 128), size)

    def cp_x(p):
        return pltpu.make_async_copy(x_hbm.at[:, cols(p * PW, PW)], hbuf.at[p], s_x.at[p])

    def cp_q(l, j):
        return pltpu.make_async_copy(wqkv_hbm.at[l, rows(j * BW, BW), :], wq.at[rows(j * BW, BW), :], s_q.at[j])

    def cp_o(l, j):
        return pltpu.make_async_copy(wo_hbm.at[l, :, cols(j * BW, BW)], wo.at[:, cols(j * BW, BW)], s_o.at[j])

    def cp_g(l, j):
        return pltpu.make_async_copy(wg_hbm.at[l, rows(j * BW, BW), :], wg.at[rows(j * BW, BW), :], s_g.at[j])

    def cp_u(l, j):
        return pltpu.make_async_copy(wu_hbm.at[l, rows(j * BW, BW), :], wu.at[rows(j * BW, BW), :], s_u.at[j])

    def cp_d(l, j):
        return pltpu.make_async_copy(wd_hbm.at[l, :, cols(j * BW, BW)], wd.at[:, cols(j * BW, BW)], s_d.at[j])

    def cp_k(l, s):
        return pltpu.make_async_copy(kc_hbm.at[l, pl.ds(s * T, T)], kv.at[s], s_kv.at[s])

    def cp_v(l, s):
        return pltpu.make_async_copy(vc_hbm.at[l, pl.ds(s * T, T)], kv.at[s], s_kv.at[s])

    scope = jax.named_scope
    barrier = pltpu.get_barrier_semaphore()
    peers = [{"tp": (tp + k) % NB} for k in range(1, NB)]
    for d in peers:
        pl.semaphore_signal(barrier, inc=1, device_id=d, device_id_type=MESH)

    lb, rb, ob = chip(3), chip(1), chip(2)
    GROUPS = ((c * R + x, (1 - c) * R + x), (c * R + lb, c * R + rb), ((1 - c) * R + lb, (1 - c) * R + rb),
              (c * R + ob, (1 - c) * R + ob))
    NG = len(GROUPS)
    blocks = [j for g in GROUPS for j in g]

    for p in range(2 * NB):
        cp_x(p).start()

    lcol = jnp.broadcast_to(len_ref[...].astype(F32), (hd, n)).T
    ang = lcol * inv_ref[...]
    lane = lax.broadcasted_iota(jnp.int32, (n, hd), 1)
    for j in blocks:
        cp_q(0, j).start()
    cosb[...] = jnp.cos(ang)
    sn = jnp.sin(ang)
    sinb[...] = jnp.where(lane < hd // 2, -sn, sn)
    for g in range(grp):
        lrow[pl.ds(g, n, stride=grp), :] = lcol

    def remote(src, dst, ss, rs, dev):
        return pltpu.make_async_remote_copy(src_ref=src, dst_ref=dst, send_sem=ss, recv_sem=rs, device_id=dev,
                                            device_id_type=MESH)

    def halves(width):
        return [(k, k + LW) for k in range(0, width, LW)]

    def put_scale(row):
        rbuf[...] = jnp.broadcast_to(row, (LW, n)).T

    def local_scale():
        def sq(p, s):
            v = hbuf[p].astype(F32)
            return s + v * v
        s = lax.fori_loop(0, 2 * NB, sq, jnp.zeros((n, PW), F32))
        r = lax.rsqrt(jnp.sum(s, axis=-1, keepdims=True) * (1.0 / D) + EPS)
        rbuf[...] = jnp.broadcast_to(r, (n, LW))

    def normalize(l, ref, j):
        for h in range(2):
            p = j * 2 + h
            for a, b in halves(PW):
                g = ref[l:l + 1, cols(p * PW + a, LW)].astype(F32)
                abuf[p, :, a:b] = (hbuf[p, :, a:b].astype(F32) * rbuf[...] * g).astype(BF16)

    def group_dot(w, js, n0, nw):
        s = None
        for j in js:
            for h in range(2):
                d = _dot(abuf[j * 2 + h], w[rows(j * BW + h * PW, PW), n0:n0 + nw])
                s = d if s is None else s + d
        return s

    def unit(i):
        return pl.ds(i * n, n)

    def tiles(width):
        return [(n0, min(256, width - n0)) for n0 in range(0, width, 256)]

    def accumulate(u, d, first):
        for k, (a, b) in enumerate(halves(d.shape[1])):
            if first:
                pool[unit(u + k), :] = d[:, a:b]
            else:
                pool[unit(u + k), :] += d[:, a:b]

    UH = n // 2

    def half_rows(u):
        return pl.ds(u * UH, UH)

    def reduce_scatter(block, wait_w, early):
        pair = []

        def other(i):
            j = (1 - c) * R + chip(RS_ORDER[i])
            wait_w(j)
            o = block(j).astype(BF16)
            part[j, 0] = o[:, :PW]
            part[j, 1] = o[:, PW:]
            d = remote(part.at[j], pair_in.at[i], pr_s.at[i], pr_r.at[i], partner)
            d.start()
            pair.append(d)

        def mine(i):
            j = c * R + chip(RS_ORDER[i])
            wait_w(j)
            o = block(j).astype(BF16)
            part[j, 0] = o[:, :PW]
            part[j, 1] = o[:, PW:]

        jo, jr, jl, jx = (c * R + chip(o) for o in RS_ORDER)
        work = [(other, 0), (other, 1), (mine, 0), (other, 2), (mine, 1), (other, 3), (mine, 2), (mine, 3)]
        with scope("rs_mm1"):
            for f, i in work[:early]:
                f(i)
        with scope("rs_wait1"):
            pair[0].wait_recv()
            m1 = []
            for h, dev in ((0, right), (1, left)):
                part[jo, h] = (part[jo, h].astype(F32) + pair_in[0, h].astype(F32)).astype(BF16)
                for u in range(2):
                    d = remote(part.at[jo, h, half_rows(u)], relay_in.at[h, half_rows(u)], rl_s.at[h * 2 + u],
                               rl_r.at[h * 2 + u], dev)
                    d.start()
                    m1.append(d)
        with scope("rs_mm2"):
            for f, i in work[early:]:
                f(i)
        with scope("rs_wait2"):
            for i, j in ((1, jr), (2, jl)):
                pair[i].wait_recv()
                for h in range(2):
                    part[j, h] = (part[j, h].astype(F32) + pair_in[i, h].astype(F32)).astype(BF16)
        with scope("rs_send2"):
            for d in m1:
                d.wait_send()
            m2 = [remote(part.at[jr, 1], rs_in.at[0], rs_s.at[0], rs_r.at[0], right),
                  remote(part.at[jl, 0], rs_in.at[1], rs_s.at[1], rs_r.at[1], left)]
            for d in m2:
                d.start()
            pair[3].wait_recv()
            for h in range(2):
                sown[h] = part[jx, h].astype(F32) + pair_in[3, h].astype(F32)
        with scope("rs_relay"):
            m3 = []
            for u in range(2):
                for h, j, dev in ((0, jr, right), (1, jl, left)):
                    m1[h * 2 + u].wait_recv()
                    ru = half_rows(u)
                    part[j, h, ru] = (part[j, h, ru].astype(F32) + relay_in[h, ru].astype(F32)).astype(BF16)
                    d = remote(part.at[j, h, ru], rs_in.at[2 + h, ru], rs_s.at[2 + h * 2 + u], rs_r.at[2 + h * 2 + u], dev)
                    d.start()
                    m3.append((h, u, d))
        own = (c * R + x) * 2
        with scope("rs_sum"):
            for h in range(2):
                m2[1 - h].wait_recv()
                sown[h] = sown[h] + rs_in[1 - h].astype(F32)
        with scope("rs_fin"):
            first = [None] * 4
            for h, u, d in m3:
                d.wait_recv()
                ru = half_rows(u)
                hbuf[own + h, ru] = (hbuf[own + h, ru].astype(F32) + (sown[h, ru] + rs_in[2 + h, ru].astype(F32))).astype(BF16)
                ref = hbuf.at[own + h, ru]
                a = remote(ref, ref, ag_s.at[h * 2 + u], ag_r.at[h * 2 + u], (right, left)[h])
                a.start()
                first[h * 2 + u] = a
        done = [d for d in pair] + m2 + [d for _, _, d in m3]
        return first, done

    def gather(first, done, stats, use):
        own = (c * R + x) * 2
        own2 = hbuf.at[pl.ds(own, 2)]
        p0 = remote(own2, own2, ad_s.at[0], ad_r.at[0], partner)
        p0.start()
        done = done + [p0]
        st = []
        with scope("stats"):
            if stats:
                q = None
                for h in range(2):
                    for a, b in halves(PW):
                        v = hbuf[own + h, :, a:b].astype(F32)
                        q = v * v if q is None else q + v * v
                sq = jnp.broadcast_to(jnp.sum(q.T, axis=0, keepdims=True), (8, n))
                stat[0] = sq
                for k in (4, 3, 5, 2, 6, 1, 7):
                    d = remote(stat.at[0], stat.at[k], st_s.at[k - 1], st_r.at[k - 1], peers[k - 1])
                    d.start()
                    st.append(d)
        with scope("ag_send2"):
            for d in first:
                d.wait_send()

            def piece(b, h):
                return hbuf.at[(c * R + b) * 2 + h]
            second = [remote(piece(x, 1), piece(x, 1), ag_s.at[4], ag_r.at[4], right),
                      remote(piece(x, 0), piece(x, 0), ag_s.at[5], ag_r.at[5], left)]
            for d in second:
                d.start()

        fw = []

        def forward(k, ref):
            d = remote(ref, ref, ad_s.at[k], ad_r.at[k], partner)
            d.start()
            fw.append(d)

        relay = []
        with scope("ag_relay"):
            for u in range(2):
                for h, b, dev in ((0, lb, right), (1, rb, left)):
                    first[h * 2 + u].wait_recv()
                    ref = hbuf.at[(c * R + b) * 2 + h, half_rows(u)]
                    d = remote(ref, ref, ag_s.at[6 + h * 2 + u], ag_r.at[6 + h * 2 + u], dev)
                    d.start()
                    relay.append(d)
                    forward(1 + h * 2 + u, ref)
        with scope("ag_stats"):
            if stats:
                for d in st:
                    d.wait_recv()
                t = stat[0]
                for k in range(1, NB):
                    t = t + stat[k]
                put_scale(lax.rsqrt(t[0:1] * (1.0 / D) + EPS))
        with scope("use0"):
            p0.wait_recv()
            use(0)
        with scope("ag_2"):
            second[0].wait_recv()
            forward(5, piece(lb, 1))
            second[1].wait_recv()
            forward(6, piece(rb, 0))
        with scope("use1"):
            use(1)
        with scope("ag_3"):
            for u in range(2):
                for h in range(2):
                    relay[u * 2 + h].wait_recv()
                    forward(7 + h * 2 + u, hbuf.at[(c * R + ob) * 2 + h, half_rows(u)])
        with scope("ag_fw1"):
            for d in fw[:6]:
                d.wait_recv()
        with scope("use2"):
            use(2)
        with scope("ag_fw2"):
            for d in fw[6:]:
                d.wait_recv()
        with scope("use3"):
            use(3)
        with scope("ag_drain"):
            for d in done + second + relay + fw + st:
                d.wait_send()

    def qkv_use(l):
        def use(g):
            js = GROUPS[g]
            for j in js:
                normalize(l, ga_ref, j)
            for j in js:
                cp_q(l, j).wait()
            for n0, nw in tiles(NQ):
                accumulate(5 * grp + n0 // LW, group_dot(wq, js, n0, nw), g == 0)
        return use

    first_row = lax.broadcasted_iota(jnp.int32, (2 * grp, S), 0) < grp
    scale = hd ** -0.5
    CH = NR // 4

    def attention(l):
        def rope(t):
            return (t * cosb[...] + pltpu.roll(t, hd // 2, 1) * sinb[...]).astype(BF16).astype(F32)

        def head(i):
            return pool[unit(5 * grp + i), :].astype(BF16).astype(F32)

        with scope("rope"):
            kn = rope(head(grp))
            vn = head(grp + 1)
            for g in range(grp):
                qrow[pl.ds(g, n, stride=grp), :] = rope(head(g))
                krow[pl.ds(g, n, stride=grp), :] = kn
                vrow[pl.ds(g, n, stride=grp), :] = vn

        def qk_step(i, carry):
            for s2 in range(SLOTS_PER_STEP):
                s = i * SLOTS_PER_STEP + s2
                cp_k(l, s).wait()
                for t in range(0, T, 2):
                    r0 = pl.multiple_of((s * T + t) * grp, 2 * grp)
                    q8 = qrow[pl.ds(r0, 2 * grp), :].astype(BF16)
                    o = _dot_nt(q8, kv[s, t:t + 2].reshape(2 * S, hd))
                    arow[pl.ds(r0, 2 * grp), :] = jnp.where(first_row, o[:, :S], o[:, S:])
            for s2 in range(SLOTS_PER_STEP):
                cp_v(l, i * SLOTS_PER_STEP + s2).start()
            return carry
        with scope("qk"):
            lax.fori_loop(0, SLOTS // SLOTS_PER_STEP, qk_step, 0)

        with scope("softmax"):
            for ch in range(4):
                rs = slice(ch * CH, (ch + 1) * CH)
                pos = lax.broadcasted_iota(jnp.int32, (CH, S), 1).astype(F32)
                sc = jnp.where(pos < lrow[rs, :], arow[rs, :] * scale, -jnp.inf)
                s_n = jnp.sum(qrow[rs, :] * krow[rs, :], axis=-1, keepdims=True) * scale
                m = jnp.maximum(jnp.max(sc, axis=-1, keepdims=True), s_n)
                p_c = jnp.exp(sc - m)
                p_n = jnp.exp(s_n - m)
                den = jnp.sum(p_c, axis=-1, keepdims=True) + p_n
                prow[rs, :] = p_c
                krow[rs, :] = jnp.broadcast_to(den, (CH, S))
                vrow[rs, :] = vrow[rs, :] * p_n

        def pv_step(i, carry):
            for s2 in range(SLOTS_PER_STEP):
                s = i * SLOTS_PER_STEP + s2
                cp_v(l, s).wait()
                for t in range(0, T, 2):
                    r0 = pl.multiple_of((s * T + t) * grp, 2 * grp)
                    p8 = prow[pl.ds(r0, 2 * grp), :]
                    pp = jnp.concatenate([jnp.where(first_row, p8, 0.0), jnp.where(first_row, 0.0, p8)], axis=1).astype(BF16)
                    arow[pl.ds(r0, 2 * grp), :] = _dot(pp, kv[s, t:t + 2].reshape(2 * S, hd))
            return carry
        with scope("pv"):
            lax.fori_loop(0, SLOTS // SLOTS_PER_STEP, pv_step, 0)

        with scope("att_out"):
            for ch in range(4):
                rs = slice(ch * CH, (ch + 1) * CH)
                arow[rs, :] = (arow[rs, :] + vrow[rs, :]) / krow[rs, :]
            for g in range(grp):
                att[:, g * hd:(g + 1) * hd] = arow[pl.ds(g, n, stride=grp), :].astype(BF16)

    def mlp_use(l):
        FU = F // LW

        def use(g):
            js = GROUPS[g]
            for j in js:
                normalize(l, gm_ref, j)
            for j in js:
                cp_g(l, j).wait()
                cp_u(l, j).wait()
            for n0, nw in tiles(F):
                if g < NG - 1:
                    for k, w in enumerate((wg, wu)):
                        accumulate((k * F + n0) // LW, group_dot(w, js, n0, nw), g == 0)
                else:
                    dg, du = group_dot(wg, js, n0, nw), group_dot(wu, js, n0, nw)
                    for k, (a, b) in enumerate(halves(nw)):
                        u = n0 // LW + k
                        gate = pool[unit(u), :] + dg[:, a:b]
                        up = pool[unit(FU + u), :] + du[:, a:b]
                        act[:, n0 + a:n0 + b] = (jax.nn.silu(gate) * up).astype(BF16)
        return use

    with scope("x_wait"):
        for p in range(2 * NB):
            cp_x(p).wait()
    with scope("scale0"):
        for s in range(SLOTS):
            cp_k(0, s).start()
        for j in range(NB):
            cp_o(0, j).start()
        local_scale()

    outs = []

    def out_use(g):
        for j in GROUPS[g]:
            for h in range(2):
                p = j * 2 + h
                d = pltpu.make_async_copy(hbuf.at[p], y_hbm.at[:, cols(p * PW, PW)], s_y.at[g * 4 + len(outs) % 4])
                d.start()
                outs.append(d)

    pending = None
    for l in range(L):
        if pending is None:
            for g in range(NG):
                with scope("qkv"):
                    qkv_use(l)(g)
        else:
            gather(*pending, True, qkv_use(l))
        attention(l)
        if l == 0:
            for j in blocks:
                cp_g(0, j).start()
                cp_u(0, j).start()
            for j in range(NB):
                cp_d(0, j).start()
            pl.semaphore_wait(barrier, NB - 1)
        pending = reduce_scatter(lambda j: _dot(att[...], wo[:, cols(j * BW, BW)]), lambda j: cp_o(l, j).wait(), 8)
        if l + 1 < L:
            for j in range(NB):
                cp_o(l + 1, j).start()
        gather(*pending, True, mlp_use(l))
        if l + 1 < L:
            for j in blocks:
                cp_q(l + 1, j).start()
            for s in range(SLOTS):
                cp_k(l + 1, s).start()
            for j in blocks:
                cp_g(l + 1, j).start()
                cp_u(l + 1, j).start()
        pending = reduce_scatter(lambda j: _dot(act[...], wd[:, cols(j * BW, BW)]), lambda j: cp_d(l, j).wait(), 3)
        if l + 1 < L:
            for j in range(NB):
                cp_d(l + 1, j).start()
    gather(*pending, False, out_use)
    with scope("y_out"):
        for d in outs:
            d.wait()


def solution(mesh):
    tp = mesh.shape["tp"]

    def body(x, g_attn, w_qkv, w_o, g_mlp, w_gate, w_up, w_down, k_cache, v_cache, lengths):
        n, D = x.shape
        L, _, NQ = w_qkv.shape
        KO, F = w_o.shape[1], w_gate.shape[2]
        S, hd = k_cache.shape[2], k_cache.shape[4]
        R = tp // 2
        NB, PW, BW = tp, D // tp // 2, D // tp
        grp = KO // hd
        kc = k_cache.reshape(L, n, S, hd)
        vc = v_cache.reshape(L, n, S, hd)
        half = hd // 2
        inv = np.float32(ROPE_THETA) ** (-np.arange(half, dtype=np.float32) * np.float32(2.0) / np.float32(hd))
        inv = jnp.asarray(np.concatenate([inv, inv])[None, :].astype(np.float32))
        dims = (L, n, D, NQ, KO, F, S, hd, R)
        anyspec = pl.BlockSpec(memory_space=pl.ANY)
        vspec = pl.BlockSpec(memory_space=pltpu.VMEM)
        V = pltpu.VMEM
        DMA = pltpu.SemaphoreType.DMA
        rows = n * grp
        scratch = [
            V((D, NQ), BF16), V((KO, D), BF16), V((D, F), BF16), V((D, F), BF16), V((F, D), BF16),
            V((SLOTS, n // SLOTS, S, hd), BF16),
            V((2 * NB, n, PW), BF16), V((2 * NB, n, PW), BF16),
            V((NB, 2, n, PW), BF16), V((R, 2, n, PW), BF16), V((2, n, PW), BF16), V((4, n, PW), BF16), V((2, n, PW), F32),
            V((max(2 * F // 128, 5 * grp + NQ // 128) * n, 128), F32), V((n, F), BF16),
            V((rows, hd), F32), V((n, hd), F32), V((n, hd), F32), V((n, KO), BF16), V((n, 128), F32), V((NB, 8, n), F32),
            DMA((2 * NB,)), DMA((NB,)), DMA((NB,)), DMA((NB,)), DMA((NB,)), DMA((NB,)), DMA((SLOTS,)), DMA((2 * NB,)),
            DMA((4,)), DMA((4,)), DMA((4,)), DMA((4,)), DMA((6,)), DMA((6,)), DMA((10,)), DMA((10,)), DMA((11,)), DMA((11,)),
            DMA((NB - 1,)), DMA((NB - 1,)),
        ]
        return pl.pallas_call(
            functools.partial(_kernel, dims),
            out_shape=jax.ShapeDtypeStruct((n, D), BF16),
            in_specs=[anyspec, vspec, anyspec, anyspec, vspec, anyspec, anyspec, anyspec, anyspec, anyspec, vspec, vspec],
            out_specs=anyspec,
            scratch_shapes=scratch,
            compiler_params=pltpu.CompilerParams(collective_id=0, has_side_effects=True, vmem_limit_bytes=67043328),
        )(x, g_attn, w_qkv, w_o, g_mlp, w_gate, w_up, w_down, kc, vc, lengths.reshape(1, n), inv)

    col = P(None, None, 'tp')
    row = P(None, 'tp', None)
    cache = P(None, 'dp', None, 'tp', None)
    return jax.shard_map(body, mesh=mesh,
                         in_specs=(P('dp', None), P(), col, row, P(), col, col, row, cache, cache, P('dp')),
                         out_specs=P('dp', None), check_vma=False)
```

time: 327 us -> 94.4 us (0.29)
  waiting for transfers between devices: 225 us -> 0 us
  Pallas kernels: 0 us -> 91.9 us
  matrix products: 71.7 us -> 0 us
  other arithmetic: 14 us -> 0 us
  between operations: 13.5 us -> 0.01 us
    psum x4 -> x0, waiting for transfers between devices: 225 us -> none  [the longest x2 114 us: body(): lax.psum(o, 'tp').astype(jnp.float32)]
    pallas_call x0 -> x1, Pallas kernels: none -> 91.9 us  [body(): pl.pallas_call(functools.partial(_kernel, dims), out_shape=jax.ShapeDtype...]
    dot_general x14 -> x0, matrix products: 71.7 us -> none  [the longest x2 25.8 us: body(): jnp.dot(act, w_down[l], preferred_element_type=jnp.float32)]
    reduce_sum x6 -> x0, other arithmetic: 7.41 us -> none  [the longest x4 6.65 us: _rmsnorm(): r = lax.rsqrt(jnp.mean(xf * xf, axis=-1, keepdims=True) + EPS)]
  transfers between devices with their start and end apart: 4 -> 0, of which waited for: 4 -> 0; matrix products, arithmetic and copies ran while one was open for 0% -> 0% of each run, Pallas kernels for 0% -> 0%
where the time goes in v2:
time: 94.4 us; the launch traced here: 94.2 us
  Pallas kernels  91.9 us (97%)
  local copies, waits for them, and re-layouts  2.29 us (2%)
    pallas_call x1, Pallas kernels, body(): pl.pallas_call(functools.partial(_kernel, dims), out_shape=jax.ShapeDtype...  91.9 us
    unnamed x1, local copies, waits for them, and re-layouts  2.29 us

profile of v2, /device:TPU:81, one launch (start us, length us, event | category | flops | bytes accessed | tf_op | source)
XLA Modules:
  0.0 94.2 jit_solution(13944022673039956124)
XLA Ops:
  0.0 91.9 %shard_map.118 = bf16[128,4096]{1,0:T(8,128)(2,1)} custom-call(bf16[128,4096]{1,0:T(8,128)(2,1)} %x_hbm.1, bf16[2,4096]{1,0:T(2,128)(2,1)} %ga_ref.1, bf16[2,4096,768]{2,1,0:T(8,128)(2,1)} %wqkv_hbm.1, bf16[2,512,4096]{2,1,0:T(8,128)(2,1)} %wo_hbm.1, bf16[2,4096]{1,0:T(2,128)(2,1)} %gm_ref.1, bf16[2,4096,1792]{2,1,0:T(8,128)(2,1)} %wg_hbm.1, ...), custom_call_target="tpu_custom_call" | custom-call | tf_op jit(solution)/shard_map/pallas_call | solution.py:520
  91.9 2.3 %copy.14 = bf16[128,4096]{1,0:T(8,128)(2,1)} copy(bf16[128,4096]{1,0:T(8,128)(2,1)} %shard_map.118) | data formatting | bytes 2097152

commit v3 on v2

--- a/solution.py
+++ b/solution.py
@@ -13,7 +13,8 @@
 F32 = jnp.float32
 BF16 = jnp.bfloat16
 SLOTS = 8
-SLOTS_PER_STEP = 2
+SLOTS_PER_STEP = 4
+U = 4
 RS_ORDER = (2, 1, 3, 0)
 
 
@@ -25,9 +26,9 @@
     return lax.dot_general(a, b, (((1,), (1,)), ((), ())), preferred_element_type=F32)
 
 
-def _kernel(dims, x_hbm, ga_ref, wqkv_hbm, wo_hbm, gm_ref, wg_hbm, wu_hbm, wd_hbm, kc_hbm, vc_hbm, len_ref, inv_ref,
+def _kernel(dims, x_hbm, ga_hbm, wqkv_hbm, wo_hbm, gm_hbm, wg_hbm, wu_hbm, wd_hbm, kc_hbm, vc_hbm, len_hbm, inv_hbm,
             y_hbm,
-            wq, wo, wg, wu, wd, kv, hbuf, abuf, part, pair_in, relay_in, rs_in, sown, pool, act, lrow, cosb, sinb, att, rbuf, stat,
+            wq, wo, wg, wu, wd, kv, hbuf, abuf, part, pair_in, relay_in, rs_in, sown, pool, act, lrow, cosb, sinb, att, rbuf, stat, ga_ref, gm_ref, len_ref, inv_ref, s_c,
             s_x, s_q, s_o, s_g, s_u, s_d, s_kv, s_y,
             pr_s, pr_r, rl_s, rl_r, rs_s, rs_r, ag_s, ag_r, ad_s, ad_r, st_s, st_r):
     L, n, D, NQ, KO, F, S, hd, R = dims
@@ -83,8 +84,6 @@
     scope = jax.named_scope
     barrier = pltpu.get_barrier_semaphore()
     peers = [{"tp": (tp + k) % NB} for k in range(1, NB)]
-    for d in peers:
-        pl.semaphore_signal(barrier, inc=1, device_id=d, device_id_type=MESH)
 
     lb, rb, ob = chip(3), chip(1), chip(2)
     GROUPS = ((c * R + x, (1 - c) * R + x), (c * R + lb, c * R + rb), ((1 - c) * R + lb, (1 - c) * R + rb),
@@ -94,17 +93,24 @@
 
     for p in range(2 * NB):
         cp_x(p).start()
-
-    lcol = jnp.broadcast_to(len_ref[...].astype(F32), (hd, n)).T
-    ang = lcol * inv_ref[...]
-    lane = lax.broadcasted_iota(jnp.int32, (n, hd), 1)
-    for j in blocks:
+    small = [pltpu.make_async_copy(a, b, s_c.at[i])
+             for i, (a, b) in enumerate(((len_hbm, len_ref), (inv_hbm, inv_ref), (ga_hbm, ga_ref), (gm_hbm, gm_ref)))]
+    for d in small:
+        d.start()
+    for j in blocks[:2]:
         cp_q(0, j).start()
-    cosb[...] = jnp.cos(ang)
-    sn = jnp.sin(ang)
-    sinb[...] = jnp.where(lane < hd // 2, -sn, sn)
-    for g in range(grp):
-        lrow[pl.ds(g, n, stride=grp), :] = lcol
+    for d in peers:
+        pl.semaphore_signal(barrier, inc=1, device_id=d, device_id_type=MESH)
+
+    def tables():
+        lcol = jnp.broadcast_to(len_ref[...].astype(F32), (hd, n)).T
+        ang = lcol * inv_ref[...]
+        lane = lax.broadcasted_iota(jnp.int32, (n, hd), 1)
+        cosb[...] = jnp.cos(ang)
+        sn = jnp.sin(ang)
+        sinb[...] = jnp.where(lane < hd // 2, -sn, sn)
+        for g in range(grp):
+            lrow[pl.ds(g, n, stride=grp), :] = lcol
 
     def remote(src, dst, ss, rs, dev):
         return pltpu.make_async_remote_copy(src_ref=src, dst_ref=dst, send_sem=ss, recv_sem=rs, device_id=dev,
@@ -152,17 +158,22 @@
             else:
                 pool[unit(u + k), :] += d[:, a:b]
 
-    UH = n // 2
+    UH = n // U
+    slow = jnp.where(x == 0, 1, 0)
+    SIDES = (slow, 1 - slow)
+    right_i, left_i = right["tp"], left["tp"]
+
+    def side_dev(h):
+        return {"tp": jnp.where(h == 0, right_i, left_i)}
 
     def half_rows(u):
         return pl.ds(u * UH, UH)
 
-    def reduce_scatter(block, wait_w, early):
+    def reduce_scatter(block, wait_w, early, then):
         pair = []
 
         def other(i):
             j = (1 - c) * R + chip(RS_ORDER[i])
-            wait_w(j)
             o = block(j).astype(BF16)
             part[j, 0] = o[:, :PW]
             part[j, 1] = o[:, PW:]
@@ -172,70 +183,92 @@
 
         def mine(i):
             j = c * R + chip(RS_ORDER[i])
-            wait_w(j)
             o = block(j).astype(BF16)
             part[j, 0] = o[:, :PW]
             part[j, 1] = o[:, PW:]
 
         jo, jr, jl, jx = (c * R + chip(o) for o in RS_ORDER)
-        work = [(other, 0), (other, 1), (mine, 0), (other, 2), (mine, 1), (other, 3), (mine, 2), (mine, 3)]
+        m1 = [remote(part.at[jo, h, half_rows(u)], relay_in.at[h, half_rows(u)], rl_s.at[h * U + u],
+                     rl_r.at[h * U + u], (right, left)[h]) for h in range(2) for u in range(U)]
+        m2 = [remote(part.at[jr, 1], rs_in.at[0], rs_s.at[0], rs_r.at[0], right),
+              remote(part.at[jl, 0], rs_in.at[1], rs_s.at[1], rs_r.at[1], left)]
+
+        def opposite(k):
+            for u in range(k * U // 2, (k + 1) * U // 2):
+                for h in range(2):
+                    ru = half_rows(u)
+                    part[jo, h, ru] = (part[jo, h, ru].astype(F32) + pair_in[0, h, ru].astype(F32)).astype(BF16)
+                    m1[h * U + u].start()
+
+        def add_pair(i, j, hs):
+            for h in hs:
+                part[j, h] = (part[j, h].astype(F32) + pair_in[i, h].astype(F32)).astype(BF16)
+
+        for j in range(NB):
+            wait_w(j)
         with scope("rs_mm1"):
-            for f, i in work[:early]:
-                f(i)
+            other(0)
+            other(1)
+            if early:
+                other(2)
+            mine(0)
         with scope("rs_wait1"):
             pair[0].wait_recv()
-            m1 = []
-            for h, dev in ((0, right), (1, left)):
-                part[jo, h] = (part[jo, h].astype(F32) + pair_in[0, h].astype(F32)).astype(BF16)
-                for u in range(2):
-                    d = remote(part.at[jo, h, half_rows(u)], relay_in.at[h, half_rows(u)], rl_s.at[h * 2 + u],
-                               rl_r.at[h * 2 + u], dev)
-                    d.start()
-                    m1.append(d)
+            opposite(0)
         with scope("rs_mm2"):
-            for f, i in work[early:]:
-                f(i)
-        with scope("rs_wait2"):
-            for i, j in ((1, jr), (2, jl)):
-                pair[i].wait_recv()
-                for h in range(2):
-                    part[j, h] = (part[j, h].astype(F32) + pair_in[i, h].astype(F32)).astype(BF16)
+            if early:
+                mine(1)
+                opposite(1)
+            else:
+                other(2)
+                opposite(1)
+                mine(1)
+            mine(2)
         with scope("rs_send2"):
-            for d in m1:
-                d.wait_send()
-            m2 = [remote(part.at[jr, 1], rs_in.at[0], rs_s.at[0], rs_r.at[0], right),
-                  remote(part.at[jl, 0], rs_in.at[1], rs_s.at[1], rs_r.at[1], left)]
-            for d in m2:
-                d.start()
-            pair[3].wait_recv()
-            for h in range(2):
-                sown[h] = part[jx, h].astype(F32) + pair_in[3, h].astype(F32)
+            pair[1].wait_recv()
+            add_pair(1, jr, (1,))
+            m2[0].start()
+            pair[2].wait_recv()
+            add_pair(2, jl, (0,))
+            m2[1].start()
+            add_pair(1, jr, (0,))
+            add_pair(2, jl, (1,))
+        with scope("rs_mm3"):
+            other(3)
+            mine(3)
+            then()
         with scope("rs_relay"):
             m3 = []
-            for u in range(2):
-                for h, j, dev in ((0, jr, right), (1, jl, left)):
-                    m1[h * 2 + u].wait_recv()
+            for u in range(U):
+                for h in SIDES:
                     ru = half_rows(u)
+                    j = jnp.where(h == 0, jr, jl)
+                    remote(relay_in.at[h, ru], relay_in.at[h, ru], rl_s.at[h * U + u], rl_r.at[h * U + u], partner).wait_recv()
                     part[j, h, ru] = (part[j, h, ru].astype(F32) + relay_in[h, ru].astype(F32)).astype(BF16)
-                    d = remote(part.at[j, h, ru], rs_in.at[2 + h, ru], rs_s.at[2 + h * 2 + u], rs_r.at[2 + h * 2 + u], dev)
+                    k = 2 + h * U + u
+                    d = remote(part.at[j, h, ru], rs_in.at[2 + h, ru], rs_s.at[k], rs_r.at[k], side_dev(h))
                     d.start()
                     m3.append((h, u, d))
         own = (c * R + x) * 2
         with scope("rs_sum"):
+            pair[3].wait_recv()
+            for h in range(2):
+                sown[h] = part[jx, h].astype(F32) + pair_in[3, h].astype(F32)
             for h in range(2):
                 m2[1 - h].wait_recv()
                 sown[h] = sown[h] + rs_in[1 - h].astype(F32)
         with scope("rs_fin"):
-            first = [None] * 4
+            first = []
             for h, u, d in m3:
                 d.wait_recv()
                 ru = half_rows(u)
                 hbuf[own + h, ru] = (hbuf[own + h, ru].astype(F32) + (sown[h, ru] + rs_in[2 + h, ru].astype(F32))).astype(BF16)
                 ref = hbuf.at[own + h, ru]
-                a = remote(ref, ref, ag_s.at[h * 2 + u], ag_r.at[h * 2 + u], (right, left)[h])
+                k = h * U + u
+                a = remote(ref, ref, ag_s.at[k], ag_r.at[k], side_dev(h))
                 a.start()
-                first[h * 2 + u] = a
-        done = [d for d in pair] + m2 + [d for _, _, d in m3]
+                first.append((h, u, a))
+        done = pair + m1 + m2 + [d for _, _, d in m3]
         return first, done
 
     def gather(first, done, stats, use):
@@ -259,13 +292,10 @@
                     d.start()
                     st.append(d)
         with scope("ag_send2"):
-            for d in first:
-                d.wait_send()
-
             def piece(b, h):
                 return hbuf.at[(c * R + b) * 2 + h]
-            second = [remote(piece(x, 1), piece(x, 1), ag_s.at[4], ag_r.at[4], right),
-                      remote(piece(x, 0), piece(x, 0), ag_s.at[5], ag_r.at[5], left)]
+            second = [remote(piece(x, 1), piece(x, 1), ag_s.at[2 * U], ag_r.at[2 * U], right),
+                      remote(piece(x, 0), piece(x, 0), ag_s.at[2 * U + 1], ag_r.at[2 * U + 1], left)]
             for d in second:
                 d.start()
 
@@ -278,14 +308,15 @@
 
         relay = []
         with scope("ag_relay"):
-            for u in range(2):
-                for h, b, dev in ((0, lb, right), (1, rb, left)):
-                    first[h * 2 + u].wait_recv()
-                    ref = hbuf.at[(c * R + b) * 2 + h, half_rows(u)]
-                    d = remote(ref, ref, ag_s.at[6 + h * 2 + u], ag_r.at[6 + h * 2 + u], dev)
-                    d.start()
-                    relay.append(d)
-                    forward(1 + h * 2 + u, ref)
+            for h, u, a in first:
+                a.wait_recv()
+                b = jnp.where(h == 0, lb, rb)
+                ref = hbuf.at[(c * R + b) * 2 + h, half_rows(u)]
+                k = 2 + 2 * U + h * U + u
+                d = remote(ref, ref, ag_s.at[k], ag_r.at[k], side_dev(h))
+                d.start()
+                relay.append((h, u, d))
+                forward(3 + h * U + u, ref)
         with scope("ag_stats"):
             if stats:
                 for d in st:
@@ -299,28 +330,27 @@
             use(0)
         with scope("ag_2"):
             second[0].wait_recv()
-            forward(5, piece(lb, 1))
+            forward(1, piece(lb, 1))
             second[1].wait_recv()
-            forward(6, piece(rb, 0))
+            forward(2, piece(rb, 0))
         with scope("use1"):
             use(1)
         with scope("ag_3"):
-            for u in range(2):
-                for h in range(2):
-                    relay[u * 2 + h].wait_recv()
-                    forward(7 + h * 2 + u, hbuf.at[(c * R + ob) * 2 + h, half_rows(u)])
+            for h, u, d in relay:
+                d.wait_recv()
+                forward(3 + 2 * U + h * U + u, hbuf.at[(c * R + ob) * 2 + h, half_rows(u)])
         with scope("ag_fw1"):
-            for d in fw[:6]:
+            for d in fw[:2 * U + 2]:
                 d.wait_recv()
         with scope("use2"):
             use(2)
         with scope("ag_fw2"):
-            for d in fw[6:]:
+            for d in fw[2 * U + 2:]:
                 d.wait_recv()
         with scope("use3"):
             use(3)
         with scope("ag_drain"):
-            for d in done + second + relay + fw + st:
+            for d in done + [d for _, _, d in first + relay] + second + fw + st:
                 d.wait_send()
 
     def qkv_use(l):
@@ -334,7 +364,15 @@
                 accumulate(5 * grp + n0 // LW, group_dot(wq, js, n0, nw), g == 0)
         return use
 
-    first_row = lax.broadcasted_iota(jnp.int32, (2 * grp, S), 0) < grp
+    quad_row = lax.broadcasted_iota(jnp.int32, (4 * grp, S), 0)
+    low = quad_row < 2 * grp
+    even = (quad_row // grp) % 2 == 0
+
+    def four(s, t):
+        a = kv[s, t:t + 2].reshape(2 * S, hd)
+        b = kv[s, t + 2:t + 4].reshape(2 * S, hd)
+        return jnp.concatenate([a, b], axis=1)
+
     scale = hd ** -0.5
     CH = NR // 4
 
@@ -353,20 +391,22 @@
                 krow[pl.ds(g, n, stride=grp), :] = kn
                 vrow[pl.ds(g, n, stride=grp), :] = vn
 
-        def qk_step(i, carry):
-            for s2 in range(SLOTS_PER_STEP):
-                s = i * SLOTS_PER_STEP + s2
-                cp_k(l, s).wait()
-                for t in range(0, T, 2):
-                    r0 = pl.multiple_of((s * T + t) * grp, 2 * grp)
-                    q8 = qrow[pl.ds(r0, 2 * grp), :].astype(BF16)
-                    o = _dot_nt(q8, kv[s, t:t + 2].reshape(2 * S, hd))
-                    arow[pl.ds(r0, 2 * grp), :] = jnp.where(first_row, o[:, :S], o[:, S:])
-            for s2 in range(SLOTS_PER_STEP):
-                cp_v(l, i * SLOTS_PER_STEP + s2).start()
-            return carry
         with scope("qk"):
-            lax.fori_loop(0, SLOTS // SLOTS_PER_STEP, qk_step, 0)
+            for s in range(SLOTS):
+                if s % SLOTS_PER_STEP == 0:
+                    for s2 in range(s, s + SLOTS_PER_STEP):
+                        cp_k(l, s2).wait()
+                for t in range(0, T, 4):
+                    r0 = (s * T + t) * grp
+                    q4 = qrow[pl.ds(r0, 4 * grp), :]
+                    q4 = jnp.concatenate([jnp.where(low, q4, 0.0), jnp.where(low, 0.0, q4)], axis=1).astype(BF16)
+                    o = _dot_nt(q4, four(s, t))
+                    arow[pl.ds(r0, 4 * grp), :] = jnp.where(even, o[:, :S], o[:, S:])
+                cp_v(l, s).start()
+
+        if l == 0:
+            for j in range(NB):
+                cp_o(0, j).start()
 
         with scope("softmax"):
             for ch in range(4):
@@ -382,18 +422,17 @@
                 krow[rs, :] = jnp.broadcast_to(den, (CH, S))
                 vrow[rs, :] = vrow[rs, :] * p_n
 
-        def pv_step(i, carry):
-            for s2 in range(SLOTS_PER_STEP):
-                s = i * SLOTS_PER_STEP + s2
-                cp_v(l, s).wait()
-                for t in range(0, T, 2):
-                    r0 = pl.multiple_of((s * T + t) * grp, 2 * grp)
-                    p8 = prow[pl.ds(r0, 2 * grp), :]
-                    pp = jnp.concatenate([jnp.where(first_row, p8, 0.0), jnp.where(first_row, 0.0, p8)], axis=1).astype(BF16)
-                    arow[pl.ds(r0, 2 * grp), :] = _dot(pp, kv[s, t:t + 2].reshape(2 * S, hd))
-            return carry
         with scope("pv"):
-            lax.fori_loop(0, SLOTS // SLOTS_PER_STEP, pv_step, 0)
+            for s in range(SLOTS):
+                if s % SLOTS_PER_STEP == 0:
+                    for s2 in range(s, s + SLOTS_PER_STEP):
+                        cp_v(l, s2).wait()
+                for t in range(0, T, 4):
+                    r0 = (s * T + t) * grp
+                    p4 = prow[pl.ds(r0, 4 * grp), :]
+                    p4 = jnp.concatenate([jnp.where(even, p4, 0.0), jnp.where(even, 0.0, p4)], axis=1).astype(BF16)
+                    o = _dot(p4, four(s, t))
+                    arow[pl.ds(r0, 4 * grp), :] = jnp.where(low, o[:, :hd], o[:, hd:])
 
         with scope("att_out"):
             for ch in range(4):
@@ -429,11 +468,11 @@
         for p in range(2 * NB):
             cp_x(p).wait()
     with scope("scale0"):
-        for s in range(SLOTS):
-            cp_k(0, s).start()
-        for j in range(NB):
-            cp_o(0, j).start()
+        for j in blocks[2:]:
+            cp_q(0, j).start()
         local_scale()
+        for d in small:
+            d.wait()
 
     outs = []
 
@@ -451,17 +490,30 @@
             for g in range(NG):
                 with scope("qkv"):
                     qkv_use(l)(g)
+                if g == 0:
+                    with scope("tables"):
+                        tables()
+                if g == 1:
+                    for s in range(SLOTS // 2):
+                        cp_k(0, s).start()
+                if g == 2:
+                    for s in range(SLOTS // 2, SLOTS):
+                        cp_k(0, s).start()
         else:
             gather(*pending, True, qkv_use(l))
         attention(l)
         if l == 0:
-            for j in blocks:
-                cp_g(0, j).start()
-                cp_u(0, j).start()
-            for j in range(NB):
-                cp_d(0, j).start()
             pl.semaphore_wait(barrier, NB - 1)
-        pending = reduce_scatter(lambda j: _dot(att[...], wo[:, cols(j * BW, BW)]), lambda j: cp_o(l, j).wait(), 8)
+
+        def mlp_weights(l=l):
+            if l == 0:
+                for j in blocks:
+                    cp_g(0, j).start()
+                    cp_u(0, j).start()
+                for j in range(NB):
+                    cp_d(0, j).start()
+
+        pending = reduce_scatter(lambda j: _dot(att[...], wo[:, cols(j * BW, BW)]), lambda j: cp_o(l, j).wait(), True, mlp_weights)
         if l + 1 < L:
             for j in range(NB):
                 cp_o(l + 1, j).start()
@@ -474,7 +526,7 @@
             for j in blocks:
                 cp_g(l + 1, j).start()
                 cp_u(l + 1, j).start()
-        pending = reduce_scatter(lambda j: _dot(act[...], wd[:, cols(j * BW, BW)]), lambda j: cp_d(l, j).wait(), 3)
+        pending = reduce_scatter(lambda j: _dot(act[...], wd[:, cols(j * BW, BW)]), lambda j: cp_d(l, j).wait(), False, lambda: None)
         if l + 1 < L:
             for j in range(NB):
                 cp_d(l + 1, j).start()
@@ -502,7 +554,6 @@
         inv = jnp.asarray(np.concatenate([inv, inv])[None, :].astype(np.float32))
         dims = (L, n, D, NQ, KO, F, S, hd, R)
         anyspec = pl.BlockSpec(memory_space=pl.ANY)
-        vspec = pl.BlockSpec(memory_space=pltpu.VMEM)
         V = pltpu.VMEM
         DMA = pltpu.SemaphoreType.DMA
         rows = n * grp
@@ -513,18 +564,21 @@
             V((NB, 2, n, PW), BF16), V((R, 2, n, PW), BF16), V((2, n, PW), BF16), V((4, n, PW), BF16), V((2, n, PW), F32),
             V((max(2 * F // 128, 5 * grp + NQ // 128) * n, 128), F32), V((n, F), BF16),
             V((rows, hd), F32), V((n, hd), F32), V((n, hd), F32), V((n, KO), BF16), V((n, 128), F32), V((NB, 8, n), F32),
+            V((L, D), BF16), V((L, D), BF16), V((1, n), jnp.int32), V((1, hd), F32), DMA((4,)),
             DMA((2 * NB,)), DMA((NB,)), DMA((NB,)), DMA((NB,)), DMA((NB,)), DMA((NB,)), DMA((SLOTS,)), DMA((2 * NB,)),
-            DMA((4,)), DMA((4,)), DMA((4,)), DMA((4,)), DMA((6,)), DMA((6,)), DMA((10,)), DMA((10,)), DMA((11,)), DMA((11,)),
+            DMA((4,)), DMA((4,)), DMA((2 * U,)), DMA((2 * U,)), DMA((2 + 2 * U,)), DMA((2 + 2 * U,)),
+            DMA((2 + 4 * U,)), DMA((2 + 4 * U,)), DMA((3 + 4 * U,)), DMA((3 + 4 * U,)),
             DMA((NB - 1,)), DMA((NB - 1,)),
         ]
-        return pl.pallas_call(
+        y = pl.pallas_call(
             functools.partial(_kernel, dims),
             out_shape=jax.ShapeDtypeStruct((n, D), BF16),
-            in_specs=[anyspec, vspec, anyspec, anyspec, vspec, anyspec, anyspec, anyspec, anyspec, anyspec, vspec, vspec],
+            in_specs=[anyspec] * 12,
             out_specs=anyspec,
             scratch_shapes=scratch,
             compiler_params=pltpu.CompilerParams(collective_id=0, has_side_effects=True, vmem_limit_bytes=67043328),
         )(x, g_attn, w_qkv, w_o, g_mlp, w_gate, w_up, w_down, kc, vc, lengths.reshape(1, n), inv)
+        return y
 
     col = P(None, None, 'tp')
     row = P(None, 'tp', None)

time: 94.4 us -> 88 us (0.932)
  Pallas kernels: 91.9 us -> 85.5 us
    pallas_call x1, Pallas kernels: 91.9 us -> 85.5 us  [body(): pl.pallas_call(functools.partial(_kernel, dims), out_shape=jax.ShapeDtype...]
where the time goes in v3:
time: 88 us; the launch traced here: 87.8 us
  Pallas kernels  85.5 us (97%)
  local copies, waits for them, and re-layouts  2.29 us (3%)
    pallas_call x1, Pallas kernels, body(): pl.pallas_call(functools.partial(_kernel, dims), out_shape=jax.ShapeDtype...  85.5 us
    unnamed x1, local copies, waits for them, and re-layouts  2.29 us

profile of v3, /device:TPU:81, one launch (start us, length us, event | category | flops | bytes accessed | tf_op | source)
XLA Modules:
  0.0 87.8 jit_solution(14483796198599671291)
XLA Ops:
  0.0 85.5 %shard_map.118 = bf16[128,4096]{1,0:T(8,128)(2,1)} custom-call(bf16[128,4096]{1,0:T(8,128)(2,1)} %x_hbm.1, bf16[2,4096]{1,0:T(2,128)(2,1)} %ga_hbm.1, bf16[2,4096,768]{2,1,0:T(8,128)(2,1)} %wqkv_hbm.1, bf16[2,512,4096]{2,1,0:T(8,128)(2,1)} %wo_hbm.1, bf16[2,4096]{1,0:T(2,128)(2,1)} %gm_hbm.1, bf16[2,4096,1792]{2,1,0:T(8,128)(2,1)} %wg_hbm.1, ...), custom_call_target="tpu_custom_call" | custom-call | tf_op jit(solution)/shard_map/pallas_call | solution.py:573
  85.5 2.3 %copy.14 = bf16[128,4096]{1,0:T(8,128)(2,1)} copy(bf16[128,4096]{1,0:T(8,128)(2,1)} %shard_map.118) | data formatting | bytes 2097152

commit v4 on v3

--- a/solution.py
+++ b/solution.py
@@ -30,7 +30,7 @@
             y_hbm,
             wq, wo, wg, wu, wd, kv, hbuf, abuf, part, pair_in, relay_in, rs_in, sown, pool, act, lrow, cosb, sinb, att, rbuf, stat, ga_ref, gm_ref, len_ref, inv_ref, s_c,
             s_x, s_q, s_o, s_g, s_u, s_d, s_kv, s_y,
-            pr_s, pr_r, rl_s, rl_r, rs_s, rs_r, ag_s, ag_r, ad_s, ad_r, st_s, st_r):
+            pr_s, pr_r, rl_s, rl_r, rs_s, rs_r, ag_s, ag_r, ad_s, ad_r, ax_s, ax_r, st_s, st_r):
     L, n, D, NQ, KO, F, S, hd, R = dims
     NB = 2 * R
     BW = D // NB
@@ -307,6 +307,18 @@
             fw.append(d)
 
         relay = []
+
+        def both_cores(h, u, ref):
+            k = h * U + u
+            return remote(ref, ref, ax_s.at[k], ax_r.at[k], {"tp": side_dev(h)["tp"] + 1 - 2 * c})
+
+        def last(h, u):
+            return hbuf.at[(c * R + ob) * 2 + h, half_rows(u)]
+
+        def last_forward(h, u):
+            k = 3 + 2 * U + h * U + u
+            return remote(last(h, u), last(h, u), ad_s.at[k], ad_r.at[k], partner)
+
         with scope("ag_relay"):
             for h, u, a in first:
                 a.wait_recv()
@@ -317,6 +329,11 @@
                 d.start()
                 relay.append((h, u, d))
                 forward(3 + h * U + u, ref)
+                extra = both_cores(h, u, ref)
+
+                @pl.when(c == 0)
+                def _():
+                    extra.start()
         with scope("ag_stats"):
             if stats:
                 for d in st:
@@ -338,20 +355,41 @@
         with scope("ag_3"):
             for h, u, d in relay:
                 d.wait_recv()
-                forward(3 + 2 * U + h * U + u, hbuf.at[(c * R + ob) * 2 + h, half_rows(u)])
+                down = last_forward(h, u)
+
+                @pl.when(c == 1)
+                def _():
+                    down.start()
         with scope("ag_fw1"):
-            for d in fw[:2 * U + 2]:
+            for d in fw:
                 d.wait_recv()
         with scope("use2"):
             use(2)
         with scope("ag_fw2"):
-            for d in fw[2 * U + 2:]:
-                d.wait_recv()
+            @pl.when(c == 0)
+            def _():
+                for h, u, _ in relay:
+                    last_forward(h, u).wait_recv()
+
+            @pl.when(c == 1)
+            def _():
+                for h, u, _ in relay:
+                    both_cores(h, u, last(h, u)).wait_recv()
         with scope("use3"):
             use(3)
         with scope("ag_drain"):
             for d in done + [d for _, _, d in first + relay] + second + fw + st:
                 d.wait_send()
+
+            @pl.when(c == 1)
+            def _():
+                for h, u, _ in relay:
+                    last_forward(h, u).wait_send()
+
+            @pl.when(c == 0)
+            def _():
+                for h, u, _ in relay:
+                    both_cores(h, u, last(h, u)).wait_send()
 
     def qkv_use(l):
         def use(g):
@@ -403,10 +441,6 @@
                     o = _dot_nt(q4, four(s, t))
                     arow[pl.ds(r0, 4 * grp), :] = jnp.where(even, o[:, :S], o[:, S:])
                 cp_v(l, s).start()
-
-        if l == 0:
-            for j in range(NB):
-                cp_o(0, j).start()
 
         with scope("softmax"):
             for ch in range(4):
@@ -470,6 +504,8 @@
     with scope("scale0"):
         for j in blocks[2:]:
             cp_q(0, j).start()
+        for s in range(SLOTS // 2):
+            cp_k(0, s).start()
         local_scale()
         for d in small:
             d.wait()
@@ -493,12 +529,12 @@
                 if g == 0:
                     with scope("tables"):
                         tables()
-                if g == 1:
-                    for s in range(SLOTS // 2):
+                if g == 0:
+                    for s in range(SLOTS // 2, SLOTS):
                         cp_k(0, s).start()
                 if g == 2:
-                    for s in range(SLOTS // 2, SLOTS):
-                        cp_k(0, s).start()
+                    for j in range(NB):
+                        cp_o(0, j).start()
         else:
             gather(*pending, True, qkv_use(l))
         attention(l)
@@ -567,7 +603,7 @@
             V((L, D), BF16), V((L, D), BF16), V((1, n), jnp.int32), V((1, hd), F32), DMA((4,)),
             DMA((2 * NB,)), DMA((NB,)), DMA((NB,)), DMA((NB,)), DMA((NB,)), DMA((NB,)), DMA((SLOTS,)), DMA((2 * NB,)),
             DMA((4,)), DMA((4,)), DMA((2 * U,)), DMA((2 * U,)), DMA((2 + 2 * U,)), DMA((2 + 2 * U,)),
-            DMA((2 + 4 * U,)), DMA((2 + 4 * U,)), DMA((3 + 4 * U,)), DMA((3 + 4 * U,)),
+            DMA((2 + 4 * U,)), DMA((2 + 4 * U,)), DMA((3 + 4 * U,)), DMA((3 + 4 * U,)), DMA((2 * U,)), DMA((2 * U,)),
             DMA((NB - 1,)), DMA((NB - 1,)),
         ]
         y = pl.pallas_call(

time: 88 us -> 85.4 us (0.970)
  Pallas kernels: 85.5 us -> 82.9 us
    pallas_call x1, Pallas kernels: 85.5 us -> 82.9 us  [body(): pl.pallas_call(functools.partial(_kernel, dims), out_shape=jax.ShapeDtype...]
where the time goes in v4:
time: 85.4 us; the launch traced here: 85.2 us
  Pallas kernels  82.9 us (97%)
  local copies, waits for them, and re-layouts  2.29 us (3%)
    pallas_call x1, Pallas kernels, body(): pl.pallas_call(functools.partial(_kernel, dims), out_shape=jax.ShapeDtype...  82.9 us
    unnamed x1, local copies, waits for them, and re-layouts  2.29 us

profile of v4, /device:TPU:81, one launch (start us, length us, event | category | flops | bytes accessed | tf_op | source)
XLA Modules:
  0.0 85.2 jit_solution(8223546899306845712)
XLA Ops:
  0.0 82.9 %shard_map.118 = bf16[128,4096]{1,0:T(8,128)(2,1)} custom-call(bf16[128,4096]{1,0:T(8,128)(2,1)} %x_hbm.1, bf16[2,4096]{1,0:T(2,128)(2,1)} %ga_hbm.1, bf16[2,4096,768]{2,1,0:T(8,128)(2,1)} %wqkv_hbm.1, bf16[2,512,4096]{2,1,0:T(8,128)(2,1)} %wo_hbm.1, bf16[2,4096]{1,0:T(2,128)(2,1)} %gm_hbm.1, bf16[2,4096,1792]{2,1,0:T(8,128)(2,1)} %wg_hbm.1, ...), custom_call_target="tpu_custom_call" | custom-call | tf_op jit(solution)/shard_map/pallas_call | solution.py:609
  82.9 2.3 %copy.14 = bf16[128,4096]{1,0:T(8,128)(2,1)} copy(bf16[128,4096]{1,0:T(8,128)(2,1)} %shard_map.118) | data formatting | bytes 2097152

commit v5 on v4

--- a/solution.py
+++ b/solution.py
@@ -97,7 +97,7 @@
              for i, (a, b) in enumerate(((len_hbm, len_ref), (inv_hbm, inv_ref), (ga_hbm, ga_ref), (gm_hbm, gm_ref)))]
     for d in small:
         d.start()
-    for j in blocks[:2]:
+    for j in blocks[:4]:
         cp_q(0, j).start()
     for d in peers:
         pl.semaphore_signal(barrier, inc=1, device_id=d, device_id_type=MESH)
@@ -215,14 +215,11 @@
         with scope("rs_wait1"):
             pair[0].wait_recv()
             opposite(0)
+            opposite(1)
         with scope("rs_mm2"):
-            if early:
-                mine(1)
-                opposite(1)
-            else:
+            if not early:
                 other(2)
-                opposite(1)
-                mine(1)
+            mine(1)
             mine(2)
         with scope("rs_send2"):
             pair[1].wait_recv()
@@ -502,7 +499,7 @@
         for p in range(2 * NB):
             cp_x(p).wait()
     with scope("scale0"):
-        for j in blocks[2:]:
+        for j in blocks[4:]:
             cp_q(0, j).start()
         for s in range(SLOTS // 2):
             cp_k(0, s).start()

time: 85.4 us -> 85.4 us (level)
  no operation moved by 1% of the time
where the time goes in v5:
time: 85.4 us; the launch traced here: 85.3 us
  Pallas kernels  83 us (97%)
  local copies, waits for them, and re-layouts  2.29 us (3%)
    pallas_call x1, Pallas kernels, body(): pl.pallas_call(functools.partial(_kernel, dims), out_shape=jax.ShapeDtype...  83 us
    unnamed x1, local copies, waits for them, and re-layouts  2.29 us

profile of v5, /device:TPU:81, one launch (start us, length us, event | category | flops | bytes accessed | tf_op | source)
XLA Modules:
  0.0 85.3 jit_solution(9427966046179986616)
XLA Ops:
  0.0 83.0 %shard_map.118 = bf16[128,4096]{1,0:T(8,128)(2,1)} custom-call(bf16[128,4096]{1,0:T(8,128)(2,1)} %x_hbm.1, bf16[2,4096]{1,0:T(2,128)(2,1)} %ga_hbm.1, bf16[2,4096,768]{2,1,0:T(8,128)(2,1)} %wqkv_hbm.1, bf16[2,512,4096]{2,1,0:T(8,128)(2,1)} %wo_hbm.1, bf16[2,4096]{1,0:T(2,128)(2,1)} %gm_hbm.1, bf16[2,4096,1792]{2,1,0:T(8,128)(2,1)} %wg_hbm.1, ...), custom_call_target="tpu_custom_call" | custom-call | tf_op jit(solution)/shard_map/pallas_call | solution.py:606
  83.0 2.3 %copy.14 = bf16[128,4096]{1,0:T(8,128)(2,1)} copy(bf16[128,4096]{1,0:T(8,128)(2,1)} %shard_map.118) | data formatting | bytes 2097152
